TPU v7x, 256 devices: a whole 4x4x8 slice. The times are simulated.
256 devices in a mesh: section: 16 (over z, x_lo), fsdp: 16 (over x_hi, y, core).
Axes of the slice: x: 4 (x_hi: 2, x_lo: 2; x = x_hi * 2 + x_lo), y: 4, z: 8, core: 2. Of those that a mesh axis runs over, the one named last changes fastest.
Arguments:
- layer_inputs: bfloat16 [16, 2, 6144, 2048], P('section', None, 'fsdp'), may hold values from -6 to 6
- out_grads: bfloat16 [16, 2, 6144, 2048], P('section', None, 'fsdp'), may hold values from -6 to 6
- attn_stash: bfloat16 [16, 2, 6144, 1024], P('section', None, 'fsdp'), may hold values from -6 to 6
- proj_grads: bfloat16 [16, 2, 6144, 1536], P('section', None, 'fsdp'), may hold values from -6 to 6
- w_qkv: bfloat16 [16, 2048, 1536], P('section', 'fsdp'), may hold values from -0.125 to 0.125
- w_out: bfloat16 [16, 1024, 2048], P('section', 'fsdp'), may hold values from -0.1875 to 0.1875
- norm_gain: float32 [16, 2048], P('section'), may hold values from 0.25 to 1.75
- b_sched: int32 [16], P('section'), may hold values from 0 to 1
- w_sched: int32 [16], P('section'), may hold values from 0 to 1
Outputs:
- prev_grads: bfloat16 [16, 6144, 2048], P('section', 'fsdp')
- grad_qkv: float32 [16, 2048, 1536], P('section', 'fsdp')
- grad_out: float32 [16, 1024, 2048], P('section', 'fsdp')
All inputs are finite; a program needn't handle non-finite values.
Results may differ from a plain program's by a relative error of at most 0.012.
Values may be sent and summed in bfloat16 or wider, within the bound.
A program may use at most 128 MiB of HBM per device.

v0:
```python
import jax
import jax.numpy as jnp
from jax import lax
from jax.sharding import Mesh
from jax.sharding import PartitionSpec as P

HEAD_DIM = 64
HEADS = 16
KV_HEADS = 4
FSDP = ("fsdp_0", "fsdp_1", "fsdp_2")


rms_eps = 1e-05
rope_base = 500000.0


def passed_along(array, axis, by):
    size = lax.axis_size(axis)
    return lax.ppermute(array, axis, [(i, (i + by) % size) for i in range(size)])


def cut_along(array, dim, size):
    before, after = (array.shape[:dim], array.shape[dim + 1 :])
    return jnp.moveaxis(array.reshape(*before, size, -1, *after), dim, 0)


def summed_rows(array, chips, core, dim):
    sizes = (lax.axis_size(chips), lax.axis_size(core))
    parts = cut_along(array, dim, sizes[0] * sizes[1])
    inside = parts.shape[1:]
    parts = parts.reshape(*sizes, *inside).swapaxes(0, 1).reshape(-1, *inside)
    parts = lax.psum_scatter(parts, core, scatter_dimension=0, tiled=True)
    return lax.psum_scatter(parts, chips, scatter_dimension=0, tiled=True)[0]


def rope_tables(length, head_size):
    halfway = head_size // 2
    indices = jnp.arange(halfway, dtype=jnp.float32)
    frequency = rope_base ** (-2.0 * indices / head_size)
    angles = jnp.arange(length, dtype=jnp.float32)[:, None] * frequency[None, :]
    angles = jnp.concatenate([angles, angles], axis=1)
    return (jnp.cos(angles), jnp.sin(angles))


def rotate_half(values):
    halfway = values.shape[-1] // 2
    return jnp.concatenate([-values[..., halfway:], values[..., :halfway]], axis=-1)


def apply_rope(values, cosine_table, sine_table):
    return values * cosine_table[:, None, :] + rotate_half(values) * sine_table[:, None, :]


def unapply_rope(values, cosine_table, sine_table):
    return values * cosine_table[:, None, :] - rotate_half(values * sine_table[:, None, :])


def contract(pattern, first_operand, second_operand):
    return jnp.einsum(pattern, first_operand, second_operand, preferred_element_type=jnp.float32)


def normalize(inputs, gain_values):
    widened = inputs.astype(jnp.float32)
    inv_rms = lax.rsqrt(jnp.mean(widened * widened, axis=-1, keepdims=True) + rms_eps)
    normed = (widened * inv_rms * gain_values).astype(jnp.bfloat16)
    return (widened, inv_rms, normed)


def attention_back(qkv_rows, attn_grad, cosine_table, sine_table):
    tokens_here = qkv_rows.shape[0]
    q_width = HEADS * HEAD_DIM
    kv_width = KV_HEADS * HEAD_DIM
    group_size = HEADS // KV_HEADS
    score_scale = HEAD_DIM ** (-0.5)
    queries = apply_rope(
        qkv_rows[:, :q_width].reshape(tokens_here, HEADS, HEAD_DIM), cosine_table, sine_table
    ).astype(jnp.bfloat16)
    key_heads = apply_rope(
        qkv_rows[:, q_width : q_width + kv_width].reshape(tokens_here, KV_HEADS, HEAD_DIM),
        cosine_table,
        sine_table,
    ).astype(jnp.bfloat16)
    values = (
        qkv_rows[:, q_width + kv_width :]
        .reshape(tokens_here, KV_HEADS, HEAD_DIM)
        .astype(jnp.bfloat16)
    )
    queries = queries.reshape(tokens_here, KV_HEADS, group_size, HEAD_DIM)
    grad_heads = attn_grad.reshape(tokens_here, KV_HEADS, group_size, HEAD_DIM)
    scores = contract("tkgd,ukd->kgtu", queries, key_heads) * score_scale
    row_ids = lax.broadcasted_iota(jnp.int32, (tokens_here, tokens_here), 0)
    col_ids = lax.broadcasted_iota(jnp.int32, (tokens_here, tokens_here), 1)
    causal = col_ids <= row_ids
    exp_scores = jnp.where(causal, jnp.exp(scores), 0.0)
    attention = exp_scores / jnp.sum(exp_scores, axis=-1, keepdims=True)
    attention_low = attention.astype(jnp.bfloat16)
    grad_values = contract("kgtu,tkgd->ukd", attention_low, grad_heads)
    grad_attention = contract("tkgd,ukd->kgtu", grad_heads, values)
    row_delta = jnp.sum(attention * grad_attention, axis=-1, keepdims=True)
    grad_scores = (attention * (grad_attention - row_delta) * score_scale).astype(jnp.bfloat16)
    grad_queries = contract("kgtu,ukd->tkgd", grad_scores, key_heads)
    grad_keys = contract("kgtu,tkgd->ukd", grad_scores, queries)
    grad_queries = unapply_rope(
        grad_queries.reshape(tokens_here, HEADS, HEAD_DIM), cosine_table, sine_table
    )
    grad_keys = unapply_rope(grad_keys, cosine_table, sine_table)
    joined = jnp.concatenate(
        [
            grad_queries.reshape(tokens_here, q_width),
            grad_keys.reshape(tokens_here, kv_width),
            grad_values.reshape(tokens_here, kv_width),
        ],
        axis=1,
    )
    return joined.astype(jnp.bfloat16)


def finish_grad(widened, inv_rms, gain_values, upstream, grad_normed):
    scaled = grad_normed * gain_values
    inner_mean = jnp.mean(scaled * widened, axis=-1, keepdims=True)
    result = upstream.astype(jnp.float32) + inv_rms * scaled - widened * inv_rms**3 * inner_mean
    return result.astype(jnp.bfloat16)


def local(
    layer_inputs, out_grads, attn_stash, proj_grads, w_qkv, w_out, norm_gain, b_sched, w_sched
):
    seq_len = layer_inputs.shape[2]
    cosine_table, sine_table = rope_tables(seq_len, HEAD_DIM)
    gain_values = norm_gain[0]
    b_slot = b_sched[0]
    w_slot = w_sched[0]
    qkv_shard = w_qkv[0]
    out_shard = w_out[0]
    contract_rows = (((0,), (0,)), ((), ()))
    contract_cols = (((1,), (1,)), ((), ()))
    inputs_b = lax.dynamic_index_in_dim(layer_inputs[0], b_slot, 0, keepdims=False)
    upstream_b = lax.dynamic_index_in_dim(out_grads[0], b_slot, 0, keepdims=False)
    widened, inv_rms, normed = normalize(inputs_b, gain_values)
    whole_qkv = lax.all_gather(qkv_shard, FSDP, axis=0, tiled=True)
    qkv_rows = jnp.dot(normed, whole_qkv, preferred_element_type=jnp.float32)
    attn_grad = lax.dot_general(
        upstream_b,
        lax.all_gather(out_shard, FSDP, axis=0, tiled=True),
        contract_cols,
        preferred_element_type=jnp.float32,
    ).astype(jnp.bfloat16)
    grad_proj = attention_back(qkv_rows, attn_grad, cosine_table, sine_table)
    grad_normed = lax.dot_general(
        grad_proj, whole_qkv, contract_cols, preferred_element_type=jnp.float32
    )
    sent_grads = finish_grad(widened, inv_rms, gain_values, upstream_b, grad_normed)
    sent_back = passed_along(sent_grads, "section", -1)[None]
    inputs_w = lax.dynamic_index_in_dim(layer_inputs[0], w_slot, 0, keepdims=False)
    upstream_w = lax.dynamic_index_in_dim(out_grads[0], w_slot, 0, keepdims=False)
    attended_w = lax.dynamic_index_in_dim(attn_stash[0], w_slot, 0, keepdims=False)
    projected_w = lax.dynamic_index_in_dim(proj_grads[0], w_slot, 0, keepdims=False)
    unused_wide, unused_inv, normed_w = normalize(inputs_w, gain_values)
    rows_part = normed_w
    grad_qkv_w = lax.psum_scatter(
        lax.dot_general(
            rows_part, projected_w, contract_rows, preferred_element_type=jnp.float32
        ).astype(jnp.bfloat16),
        FSDP,
        scatter_dimension=0,
        tiled=True,
    ).astype(jnp.float32)
    rows_part = attended_w
    grad_out_w = summed_rows(
        lax.dot_general(
            rows_part, upstream_w, contract_rows, preferred_element_type=jnp.float32
        ).astype(jnp.bfloat16),
        ("fsdp_0", "fsdp_1"),
        "fsdp_2",
        0,
    ).astype(jnp.float32)
    grad_qkv_w, grad_out_w = (grad_qkv_w[None], grad_out_w[None])
    return (sent_back, grad_qkv_w, grad_out_w)


def solution(mesh):
    finer = Mesh(
        mesh.devices.reshape(mesh.shape["section"], 2, 4, 2),
        ("section", "fsdp_0", "fsdp_1", "fsdp_2"),
    )
    return jax.shard_map(
        local,
        mesh=finer,
        in_specs=(
            P("section", None, FSDP, None),
            P("section", None, FSDP, None),
            P("section", None, FSDP, None),
            P("section", None, FSDP, None),
            P("section", FSDP, None),
            P("section", FSDP, None),
            P("section", None),
            P("section"),
            P("section"),
        ),
        out_specs=(P("section", FSDP, None), P("section", FSDP, None), P("section", FSDP, None)),
        check_vma=False,
    )
```

profile of v0, /device:TPU:97, one launch (start us, length us, event | category | flops | bytes accessed | tf_op | source)
XLA Modules:
  0.0 279.0 jit_solution(17291368382302800708)
XLA Ops:
  8.0 0.0 copy-start
  8.0 0.0 all-gather.7.cloned.1.call-start
  8.1 0.7 all-gather.7.cloned.1.call-update
  8.7 0.0 reduce-scatter.6.cloned.1.call-start
  9.4 4.0 %convolution_convert_fusion.1 = bf16[1024,2048]{1,0:T(8,128)(2,1)S(1)} fusion(bf16[1,2,384,2048]{3,2,1,0:T(8,128)(2,1)} %param.10, s32[]{:T(128)S(6)} %select_n.19, bf16[1,2,384,1024]{3,2,1,0:T(8,128)(2,1)} %param.11), kind=kOutput, calls=%fused_computation.27 | convolution fusion | flops 1612709888 | bytes 6554624 | tf_op jit(solution)/shard_map/dot_general | solution.py:170
  13.5 2.3 copy.33
  15.8 0.0 reduce-scatter.6.cloned.1.call-update
  15.8 0.0 all-gather.5.cloned.1.call-start
  15.9 0.7 all-gather.5.cloned.1.call-update
  16.6 0.0 reduce-scatter.4.cloned.1.call-start
  16.6 1.8 fusion.17
  18.4 0.0 copy-done
  18.4 0.0 copy-done.17
  18.4 7.2 %convolution_convert_fusion = bf16[2048,1536]{1,0:T(8,128)(2,1)} fusion(f32[2048]{0:T(1024)S(1)} %bitcast.182, f32[384]{0:T(512)S(1)} %add_rsqrt_fusion, bf16[1,2,384,2048]{3,2,1,0:T(8,128)(2,1)} %param.9, s32[]{:T(128)S(6)} %select_n.19, bf16[1,2,384,1536]{3,2,1,0:T(8,128)(2,1)S(1)} %copy-done), kind=kOutput, calls=%fused_computation.9 | convolution fusion | flops 2422210560 | bytes 9055232 | tf_op jit(solution)/shard_map/dot_general | solution.py:161
  25.6 0.0 reduce-scatter.4.cloned.1.call-update
  25.7 0.0 reduce-scatter.8.cloned.1.call-start
  26.4 1.8 fusion.20
  28.2 0.7 iota_compare_fusion
  28.9 0.1 iota_multiply_fusion
  29.0 0.9 fusion.74
  29.8 43.9 %all-gather.7.cloned.1.call-done = bf16[1,1024,2048]{2,1,0:T(8,128)(2,1)} async-done(((bf16[1,64,2048]{2,1,0:T(8,128)(2,1)}), bf16[1,1024,2048]{2,1,0:T(8,128)(2,1)}) %all-gather.7.cloned.1.call-update) | async-done | bytes 4194320 | tf_op jit(solution)/shard_map/all_gather | solution.py:144
  73.7 4.5 %fusion.45 = bf16[384,1024]{1,0:T(8,128)(2,1)S(1)} fusion(bf16[1,1024,2048]{2,1,0:T(8,128)(2,1)} %all-gather.7.cloned.1.call-done, bf16[1,2,384,2048]{3,2,1,0:T(8,128)(2,1)} %param.10, s32[]{:T(128)S(6)} %select_n.17), kind=kOutput, calls=%fused_computation.56 | convolution fusion | flops 1611005952 | bytes 6553604 | tf_op jit(solution)/shard_map/dot_general | solution.py:142
  78.2 0.4 copy.29
  78.6 0.0 reduce-scatter.6.cloned.1.call-done
  78.6 0.0 reduce-scatter.8.cloned.1.call-update
  78.7 79.5 %all-gather.5.cloned.1.call-done = bf16[1,2048,1536]{2,1,0:T(8,128)(2,1)} async-done(((bf16[1,128,1536]{2,1,0:T(8,128)(2,1)}), bf16[1,2048,1536]{2,1,0:T(8,128)(2,1)}) %all-gather.5.cloned.1.call-update) | async-done | bytes 6291472 | tf_op jit(solution)/shard_map/all_gather | solution.py:140
  158.2 5.3 %fusion.8 = f32[384,1536]{1,0:T(8,128)S(1)} fusion(bf16[1,2048,1536]{2,1,0:T(8,128)(2,1)} %all-gather.5.cloned.1.call-done, f32[2048]{0:T(1024)S(1)} %bitcast.183, f32[384]{0:T(512)S(1)} %get-tuple-element.14, bf16[1,2,384,2048]{3,2,1,0:T(8,128)(2,1)} %param.9, s32[]{:T(128)S(6)} %select_n.17), kind=kOutput, calls=%fused_computation.12 | convolution fusion | flops 2419064832 | bytes 10233348 | tf_op jit(solution)/shard_map/dot_general | solution.py:141
  163.5 1.3 slice.48
  164.8 0.7 slice.61
  165.5 0.2 copy.25
  165.6 0.8 slice_negate_fusion.3
  166.4 1.9 copy.26
  168.3 1.0 slice_negate_fusion.1
  169.3 1.7 copy.28
  171.1 0.0 copy-start.4
  171.1 6.1 %fusion.89 = f32[4,384,384,4]{2,1,3,0:T(8,128)} fusion(bf16[384,4,64,1]{0,2,3,1:T(8,128)(2,1)} %bitcast.178, bf16[384,4,4,64]{0,3,2,1:T(8,128)(2,1)S(1)} %bitcast.171), kind=kOutput, calls=%fused_computation.104 | convolution fusion | flops 301989888 | bytes 10420224 | tf_op jit(solution)/shard_map/tkgd,ukd->kgtu/dot_general | solution.py:59
  177.2 0.0 copy-done.5
  177.2 0.1 fusion.72
  177.3 0.0 copy-start.13
  177.3 0.3 fusion.34
  177.6 0.5 copy-done.15
  178.1 5.8 %fusion.5 = (f32[4,4,384]{2,1,0:T(4,128)S(1)}, f32[4,384,384,4]{2,1,3,0:T(8,128)}) fusion(pred[384,384]{0,1:T(8,128)(4,1)S(1)} %copy-done.15, bf16[384,4,64,1]{0,2,3,1:T(8,128)(2,1)S(1)} %fusion.72, bf16[384,4,4,64]{0,3,2,1:T(8,128)(2,1)S(1)} %fusion.34), kind=kOutput, calls=%fused_computation.8 | convolution fusion | flops 309061632 | bytes 10592256 | tf_op jit(solution)/shard_map/tkgd,ukd->kgtu/dot_general | solution.py:59
  183.9 0.0 copy-start.14
  183.9 18.0 %broadcast_multiply_fusion = (f32[384,4,64]{0,2,1:T(8,128)S(1)}, f32[384,4,64]{0,2,1:T(8,128)S(1)}) fusion(f32[384,64]{0,1:T(8,128)S(1)} %copy-done.8, bf16[384,4,4,64]{0,3,2,1:T(8,128)(2,1)} %copy-done.12, f32[4,384,384,4]{2,1,3,0:T(8,128)} %fusion.89, f32[4,4,384]{2,1,0:T(4,128)S(1)} %get-tuple-element.15, f32[4,384,384,4]{2,1,3,0:T(8,128)} %get-tuple-element.16, ...), kind=kOutput, calls=%fused_computation.85 | convolution fusion | flops 328046976 | bytes 20717568 | tf_op jit(solution)/shard_map/kgtu,tkgd->ukd/dot_general | solution.py:59
  201.9 16.2 %fusion.16 = f32[4,64,4,384]{3,1,2,0:T(8,128)} fusion(bf16[384,4,64,1]{0,2,3,1:T(8,128)(2,1)S(1)} %copy-done.14, f32[4,384,384,4]{2,1,3,0:T(8,128)} %fusion.89, f32[4,384,384,4]{2,1,3,0:T(8,128)} %get-tuple-element.16, f32[4,4,384]{2,1,0:T(4,128)S(1)} %get-tuple-element.15, pred[384,384]{0,1:T(8,128)(4,1)S(1)} %copy-done.16), kind=kOutput, calls=%fused_computation.24 | convolution fusion | flops 327948672 | bytes 20815872 | tf_op jit(solution)/shard_map/kgtu,ukd->tkgd/dot_general | solution.py:59
  218.2 1.5 bitcast_multiply_fusion.8
  219.7 0.0 copy-start.3
  219.7 0.1 slice_negate_fusion
  219.9 0.1 pad_maximum_fusion
  220.0 1.2 copy-done.3
  221.1 0.3 fusion.36
  221.4 0.1 fusion.71
  221.5 0.0 copy-start.2
  221.5 0.0 slice-start.1
  221.5 6.2 %fusion.63 = bf16[4,64,384]{2,1,0:T(8,128)(2,1)S(1)} fusion(bf16[384,4,4,64]{0,3,2,1:T(8,128)(2,1)S(1)} %bitcast.172, f32[4,384,384,4]{2,1,3,0:T(8,128)} %get-tuple-element.16, f32[4,4,384]{2,1,0:T(4,128)S(1)} %get-tuple-element.15, pred[384,384]{0,1:T(8,128)(4,1)S(1)} %copy-done.16), kind=kOutput, calls=%fused_computation.68 | convolution fusion | flops 311525376 | bytes 10592256 | tf_op jit(solution)/shard_map/kgtu,tkgd->ukd/dot_general | solution.py:59
  227.8 0.0 copy-start.11
  227.8 2.8 %fusion.26 = (f32[384]{0:T(512)S(1)}, f32[384,2048]{1,0:T(8,128)S(1)}) fusion(bf16[1,2,384,2048]{3,2,1,0:T(8,128)(2,1)S(1)} %copy-done.2, s32[]{:T(128)S(6)} %select_n.17, f32[2048]{0:T(1024)S(1)} %bitcast.184, bf16[1,2048,1536]{2,1,0:T(8,128)(2,1)S(1)} %bitcast.181, bf16[384,256]{0,1:T(8,128)(2,1)S(1)} %bitcast.185, bf16[384,256]{0,1:T(8,128)(2,1)S(1)} %bitcast.179, ...), kind=kOutput, calls=%fused_computation.37 | convolution fusion | flops 2422603264 | bytes 12199428 | tf_op jit(solution)/shard_map/dot_general | solution.py:149
  230.6 0.0 copy-start.1
  230.6 2.0 fusion.25
  232.7 0.2 collective-permute-start
  232.9 2.0 bitcast_convert_fusion
  234.8 1.8 convert_element_type.74
  236.6 32.1 %collective-permute-done = bf16[384,2048]{1,0:T(8,128)(2,1)} collective-permute-done((bf16[384,2048]{1,0:T(8,128)(2,1)}, bf16[384,2048]{1,0:T(8,128)(2,1)}, u32[]{:S(2)}, u32[]{:S(2)}) %collective-permute-start) | collective-permute-done | bytes 1572896 | tf_op jit(solution)/shard_map/ppermute | solution.py:19
  268.7 2.7 copy.44
  (35 shorter events, 0.1 us)
Async XLA Ops:
  8.0 10.4 %copy-start = (bf16[1,2,384,1536]{3,2,1,0:T(8,128)(2,1)S(1)}, bf16[1,2,384,1536]{3,2,1,0:T(8,128)(2,1)}, u32[]{:S(2)}) copy-start(bf16[1,2,384,1536]{3,2,1,0:T(8,128)(2,1)} %param.12) | copy-start | bytes 7077892
  8.0 65.7 %all-gather.7.cloned.1.call-start = ((), (), s32[]{:S(2)}) async-start(), calls=%async_computation.7 | async-start | bytes 4456448 | tf_op jit(solution)/shard_map/all_gather | solution.py:144
  8.7 69.9 %reduce-scatter.6.cloned.1.call-start = ((), (), s32[]{:S(2)}) async-start(), calls=%async_computation.4 | async-start | bytes 6291456 | tf_op jit(solution)/shard_map/reduce_scatter | solution.py:32
  15.8 2.6 copy-start.17
  15.8 142.4 %all-gather.5.cloned.1.call-start = ((), (), s32[]{:S(2)}) async-start(), calls=%async_computation.6 | async-start | bytes 6684672 | tf_op jit(solution)/shard_map/all_gather | solution.py:140
  16.6 216.3 %reduce-scatter.4.cloned.1.call-start = ((), (), s32[]{:S(2)}) async-start(), calls=%async_computation.3 | async-start | bytes 6684672 | tf_op jit(solution)/shard_map/reduce_scatter | solution.py:160
  25.7 209.2 %reduce-scatter.8.cloned.1.call-start = ((), (), s32[]{:S(2)}) async-start(), calls=%async_computation.5 | async-start | bytes 2359296 | tf_op jit(solution)/shard_map/reduce_scatter | solution.py:33
  171.1 6.2 %copy-start.5 = (f32[384,64]{0,1:T(8,128)S(1)}, f32[384,64]{0,1:T(8,128)}, u32[]{:S(2)}) copy-start(f32[384,64]{0,1:T(8,128)} %get-tuple-element.11) | copy-start | bytes 294916
  171.1 6.2 %copy-start.7 = (f32[384,64]{0,1:T(8,128)S(1)}, f32[384,64]{0,1:T(8,128)}, u32[]{:S(2)}) copy-start(f32[384,64]{0,1:T(8,128)} %get-tuple-element.12) | copy-start | bytes 294916
  171.1 6.2 %copy-start.9 = (f32[384,4,32]{0,2,1:T(8,128)S(1)}, f32[384,4,32]{0,2,1:T(8,128)}, u32[]{:S(2)}) copy-start(f32[384,4,32]{0,2,1:T(8,128)} %get-tuple-element.9) | copy-start | bytes 589828
  171.1 6.2 %copy-start.10 = (f32[384,4,32]{0,2,1:T(8,128)S(1)}, f32[384,4,32]{0,2,1:T(8,128)}, u32[]{:S(2)}) copy-start(f32[384,4,32]{0,2,1:T(8,128)} %get-tuple-element.10) | copy-start | bytes 589828
  171.1 6.2 %copy-start.4 = (f32[384,16,32]{0,2,1:T(8,128)S(1)}, f32[384,16,32]{0,2,1:T(8,128)}, u32[]{:S(2)}) copy-start(f32[384,16,32]{0,2,1:T(8,128)} %get-tuple-element.6) | copy-start | bytes 2359300
  177.2 0.9 copy-start.15
  177.3 6.6 %copy-start.13 = (bf16[384,4,64,1]{0,2,3,1:T(8,128)(2,1)}, bf16[384,4,64,1]{0,2,3,1:T(8,128)(2,1)S(1)}, u32[]{:S(2)}) copy-start(bf16[384,4,64,1]{0,2,3,1:T(8,128)(2,1)S(1)} %fusion.72) | copy-start | bytes 589828
  178.1 5.8 %copy-start.12 = (bf16[384,4,4,64]{0,3,2,1:T(8,128)(2,1)}, bf16[384,4,4,64]{0,3,2,1:T(8,128)(2,1)S(1)}, u32[]{:S(2)}) copy-start(bf16[384,4,4,64]{0,3,2,1:T(8,128)(2,1)S(1)} %fusion.34) | copy-start | bytes 2359300
  178.1 5.8 %copy-start.8 = (f32[384,64]{0,1:T(8,128)S(1)}, f32[384,64]{0,1:T(8,128)}, u32[]{:S(2)}) copy-start(f32[384,64]{0,1:T(8,128)} %get-tuple-element.12) | copy-start | bytes 294916
  178.1 5.8 %copy-start.16 = (pred[384,384]{0,1:T(8,128)(4,1)S(1)}, pred[384,384]{0,1:T(8,128)(4,1)}, u32[]{:S(2)}) copy-start(pred[384,384]{0,1:T(8,128)(4,1)} %iota_compare_fusion) | copy-start | bytes 442372
  183.9 18.0 %copy-start.14 = (bf16[384,4,64,1]{0,2,3,1:T(8,128)(2,1)S(1)}, bf16[384,4,64,1]{0,2,3,1:T(8,128)(2,1)}, u32[]{:S(2)}) copy-start(bf16[384,4,64,1]{0,2,3,1:T(8,128)(2,1)} %copy-done.13) | copy-start | bytes 589828
  219.7 1.4 copy-start.3
  219.7 1.4 copy-start.6
  221.1 6.6 %slice-start = ((s8[6291456]{0:T(1024)(128)(4,1)}), s8[4194304]{0:T(1024)(128)(4,1)S(1)}, s32[]{:S(2)}) async-start(s8[6291456]{0:T(1024)(128)(4,1)} %bitcast.180), calls=%async_computation.8 | async-start | bytes 8388608
  221.5 6.3 %copy-start.2 = (bf16[1,2,384,2048]{3,2,1,0:T(8,128)(2,1)S(1)}, bf16[1,2,384,2048]{3,2,1,0:T(8,128)(2,1)}, u32[]{:S(2)}) copy-start(bf16[1,2,384,2048]{3,2,1,0:T(8,128)(2,1)} %param.9) | copy-start | bytes 9437188
  221.5 6.3 %slice-start.1 = ((s8[6291456]{0:T(1024)(128)(4,1)}), s8[2097152]{0:T(1024)(128)(4,1)S(1)}, s32[]{:S(2)}) async-start(s8[6291456]{0:T(1024)(128)(4,1)} %bitcast.180), calls=%async_computation.9 | async-start | bytes 4194304
  227.8 2.8 %copy-start.11 = (bf16[1,2,384,2048]{3,2,1,0:T(8,128)(2,1)S(1)}, bf16[1,2,384,2048]{3,2,1,0:T(8,128)(2,1)}, u32[]{:S(2)}) copy-start(bf16[1,2,384,2048]{3,2,1,0:T(8,128)(2,1)} %param.10) | copy-start | bytes 9437188
  230.6 40.8 %copy-start.1 = (bf16[1,2,384,1536]{3,2,1,0:T(8,128)(2,1)S(1)}, bf16[1,2,384,1536]{3,2,1,0:T(8,128)(2,1)}, u32[]{:S(2)}) copy-start(bf16[1,2,384,1536]{3,2,1,0:T(8,128)(2,1)} %param.12) | copy-start | bytes 7077892
  232.7 36.0 %collective-permute-start = (bf16[384,2048]{1,0:T(8,128)(2,1)}, bf16[384,2048]{1,0:T(8,128)(2,1)}, u32[]{:S(2)}, u32[]{:S(2)}) collective-permute-start(bf16[384,2048]{1,0:T(8,128)(2,1)} %fusion.25), channel_id=1, source_target_pairs={{0,240},{16,0},{32,16},{48,32},{64,48},{80,64},{96,80},{112,96},{1... | collective-permute-start | bytes 4718600 | tf_op jit(solution)/shard_map/ppermute | solution.py:19
Sparse Core Ops, SparseCore 0:
  11.6 62.1 all-gather.6
  76.5 81.6 all-gather.4
Sparse Core Ops, SparseCore 1:
  15.9 19.6 reduce-scatter.5
  39.9 100.0 reduce-scatter.3
  143.8 81.1 reduce-scatter.7
where the time goes:
time: 282 us; the launch traced here: 279 us
  waiting for transfers between devices  157 us (56%)
  matrix products  76.1 us (27%)
  between operations  17.3 us (6%)
  other arithmetic  15.3 us (5%)
  local copies, waits for them, and re-layouts  12.9 us (5%)
    all_gather x1, waiting for transfers between devices, local(): whole_qkv = lax.all_gather(qkv_shard, FSDP, axis=0, tiled=True)  79.5 us
    dot_general x5, matrix products, contract(): jnp.einsum(pattern, first_operand, second_operand, preferred_element_type...  52.3 us
    all_gather x1, waiting for transfers between devices, local(): lax.all_gather(out_shard, FSDP, axis=0, tiled=True)  43.9 us
    ppermute x1, waiting for transfers between devices, passed_along(): lax.ppermute(array, axis, [(i, (i + by) % size) for i in range(size)])  32.1 us
    dot_general x1, matrix products, local(): lax.dot_general(rows_part, projected_w, contract_rows, preferred_element_...  7.19 us
  transfers between devices with their start and end apart: 6, of which 3 were waited for; matrix products, arithmetic and copies ran while one was open for 36% of the time, Pallas kernels for 0%

commit v1 on v0

v1 whole, which is shorter than its diff:
```python
import functools

import jax
import jax.numpy as jnp
import numpy as np
from jax import lax
from jax.experimental import pallas as pl
from jax.experimental.pallas import tpu as pltpu
from jax.sharding import PartitionSpec as P

D = 2048
HEAD_DIM = 64
HEADS = 16
KV_HEADS = 4
SEQ = 384
QW = 1024
QKVW = 1536
CHIPS = 8
EPS = 1e-05
SCALE = HEAD_DIM ** (-0.5)
BF = jnp.bfloat16
F32 = jnp.float32
MESH = pl.DeviceIdType.MESH

Q_X, Q_YP, Q_YM, Q_PP, Q_PM, Q_RO, Q_RP = range(7)
O_YP, O_YM, O_X0, O_XP, O_XM, O_X2, O_RA, O_RB = range(7, 15)
SIB_Q = 15
SIB_O = 23
RS_SIB_Q, RS_SIB_O = 31, 32
R1_Q, R1_O = 33, 35
R2_Q, R2_O = 37, 41
RX_Q, RX_O = 45, 46
PERM = 47
N_SEM = 50


def rope_tables():
    half = HEAD_DIM // 2
    freq = 500000.0 ** (-2.0 * np.arange(half) / HEAD_DIM)
    ang = np.arange(SEQ)[:, None] * freq[None, :]
    cos = np.tile(np.cos(ang), (1, 4)).astype(np.float32)
    sin = np.tile(np.sin(ang), (1, 4)).astype(np.float32)
    sign = np.where(np.arange(128) % 64 < 32, -1.0, 1.0).astype(np.float32)
    return cos, sin * sign[None, :]


def dot(a, b, ca, cb):
    return lax.dot_general(a, b, (((ca,), (cb,)), ((), ())), preferred_element_type=F32)


def kernel(
    x_hbm, g_hbm, a_hbm, p_hbm, wq_hbm, wo_hbm, gain_ref, b_ref, w_ref, cos_ref, sin_ref,
    prev_hbm, gq_ref, go_ref,
    X, G, A, PG, WQ, WO, DQ, DO, SQ, SO, R1Q, R1O, R2Q, R2O, RXQ, RXO,
    N, INV, Q, KD, VD, AGR, GP, DKD, DVD, U, DOT, OUT,
    lsem, ssem, rsem,
):
    s = lax.axis_index("section")
    f = lax.axis_index("fsdp")
    xh, y, c = f // 8, (f // 2) % 4, f % 2
    up, down, far = (y + 1) % 4, (y + 3) % 4, (y + 2) % 4
    oc, ox = 1 - c, 1 - xh
    n_sec = lax.axis_size("section")

    def dev(xx, yy, cc):
        return (s, xx * 8 + yy * 2 + cc)

    d_up, d_down, d_x, d_sib = dev(xh, up, c), dev(xh, down, c), dev(ox, y, c), dev(xh, y, oc)
    d_prev, d_next = (lax.rem(s + n_sec - 1, n_sec), f), (lax.rem(s + 1, n_sec), f)

    def qs(ref, xx, yy, cc):
        return ref.at[xx * 4 + yy, pl.ds(pl.multiple_of(cc * 128, 128), 128), :]

    def os(ref, xx, yy, cc, lo=0, n=64):
        return ref.at[xx * 4 + yy, pl.ds(pl.multiple_of(cc * 64 + lo, 32), n), :]

    started = []

    def rcopy(src, dst, slot, device):
        return pltpu.make_async_remote_copy(
            src_ref=src, dst_ref=dst, send_sem=ssem.at[slot], recv_sem=rsem.at[slot],
            device_id=device, device_id_type=MESH,
        )

    def send(src, dst, slot, device):
        cp = rcopy(src, dst, slot, device)
        cp.start()
        started.append(cp)

    def recv(dst, slot):
        rcopy(dst, dst, slot, d_sib).wait_recv()

    def gather(ref, shard, slot, device, src=None):
        send(shard if src is None else src, shard, slot, device)

    barrier = pltpu.get_barrier_semaphore()
    for d in (d_up, d_down, d_x, d_sib, d_prev, d_next):
        pl.semaphore_signal(barrier, inc=1, device_id=d, device_id_type=MESH)
    loads = [
        pltpu.make_async_copy(g_hbm, G, lsem.at[0]),
        pltpu.make_async_copy(a_hbm, A, lsem.at[1]),
        pltpu.make_async_copy(x_hbm, X, lsem.at[2]),
        pltpu.make_async_copy(p_hbm, PG, lsem.at[3]),
        pltpu.make_async_copy(wq_hbm, qs(WQ, xh, y, c), lsem.at[4]),
        pltpu.make_async_copy(wo_hbm, os(WO, xh, y, c), lsem.at[5]),
    ]
    for cp in (loads[4], loads[5], loads[0], loads[1], loads[2], loads[3]):
        cp.start()
    pl.semaphore_wait(barrier, 6)

    mine_q, mine_o = qs(WQ, xh, y, c), os(WO, xh, y, c)
    gather(WQ, mine_q, Q_X, d_x, wq_hbm)
    gather(WQ, mine_q, Q_YP, d_up, wq_hbm)
    gather(WQ, mine_q, Q_YM, d_down, wq_hbm)
    gather(WO, mine_o, O_YP, d_up, wo_hbm)
    gather(WO, mine_o, O_YM, d_down, wo_hbm)
    gather(WO, mine_o, O_X0, d_x, wo_hbm)
    gather(WQ, mine_q, SIB_Q + 0, d_sib, wq_hbm)
    gather(WO, mine_o, SIB_O + 0, d_sib, wo_hbm)

    b_slot, w_slot = b_ref[0], w_ref[0]

    loads[0].wait()
    loads[1].wait()

    def out_part(j, carry):
        lhs = A[w_slot, :, pl.ds(pl.multiple_of(j * 256, 256), 256)]

        def cols(n, carry):
            sl = pl.ds(pl.multiple_of(n * 512, 512), 512)
            part = dot(lhs, G[w_slot, :, sl], 0, 0).astype(BF)
            DO[pl.ds(2 * j, 2), :, sl] = part.reshape(2, 128, 512)
            return carry

        return lax.fori_loop(0, 4, cols, carry)

    lax.fori_loop(0, 4, out_part, 0)
    loads[2].wait()
    loads[3].wait()

    def norm(slot):
        def rows(r, carry):
            sl = pl.ds(pl.multiple_of(r * 16, 16), 16)
            wide = X[slot, sl, :].astype(F32)
            inv = lax.rsqrt(jnp.mean(wide * wide, axis=-1, keepdims=True) + EPS)
            INV[sl, :] = jnp.broadcast_to(inv, (16, 128))
            N[sl, :] = (wide * inv * gain_ref[...]).astype(BF)
            return carry

        lax.fori_loop(0, SEQ // 16, rows, 0)

    norm(w_slot)

    def qkv_part(j, carry):
        lhs = N[:, pl.ds(pl.multiple_of(j * 256, 256), 256)]

        def cols(n, carry):
            sl = pl.ds(pl.multiple_of(n * 512, 512), 512)
            DQ[j, :, sl] = dot(lhs, PG[w_slot, :, sl], 0, 0).astype(BF)
            return carry

        return lax.fori_loop(0, 3, cols, carry)

    lax.fori_loop(0, CHIPS, qkv_part, 0)
    norm(b_slot)
    send(DQ.at[:, pl.ds(pl.multiple_of(oc * 128, 128), 128), :], SQ, RS_SIB_Q, d_sib)
    send(DO.at[:, pl.ds(pl.multiple_of(oc * 64, 64), 64), :], SO, RS_SIB_O, d_sib)

    sgn = 1 - 2 * xh
    ya, yb = (y + 4 - sgn) % 4, (y + 4 + sgn) % 4
    part_q = qs(WQ, ox, y, c)
    recv(part_q, Q_X)
    gather(WQ, part_q, Q_PP, d_up)
    gather(WQ, part_q, Q_PM, d_down)
    gather(WQ, part_q, SIB_Q + 1, d_sib)
    from_down, from_up = qs(WQ, xh, down, c), qs(WQ, xh, up, c)
    recv(from_down, Q_YP)
    recv(from_up, Q_YM)
    gather(WQ, from_down, SIB_Q + 2, d_sib)
    gather(WQ, from_up, SIB_Q + 3, d_sib)
    o_down, o_up = os(WO, xh, down, c), os(WO, xh, up, c)
    recv(o_down, O_YP)
    recv(o_up, O_YM)
    gather(WO, os(WO, xh, down, c, 0, 32), O_RA, d_up)
    gather(WO, os(WO, xh, up, c, 32, 32), O_RB, d_down)
    gather(WO, o_down, O_XP, d_x)
    gather(WO, o_up, O_XM, d_x)
    gather(WO, o_down, SIB_O + 1, d_sib)
    gather(WO, o_up, SIB_O + 2, d_sib)
    gather(WQ, qs(WQ, xh, ya, c), Q_RO, dev(xh, yb, c))

    recv(SQ, RS_SIB_Q)
    recv(SO, RS_SIB_O)

    def pair_sum(j, carry):
        sq = pl.ds(pl.multiple_of(c * 128, 128), 128)
        so = pl.ds(pl.multiple_of(c * 64, 64), 64)
        DQ[j, sq, :] = (DQ[j, sq, :].astype(F32) + SQ[j].astype(F32)).astype(BF)
        DO[j, so, :] = (DO[j, so, :].astype(F32) + SO[j].astype(F32)).astype(BF)
        return carry

    lax.fori_loop(0, CHIPS, pair_sum, 0)

    part_down, part_up = qs(WQ, ox, down, c), qs(WQ, ox, up, c)
    recv(part_down, Q_PP)
    recv(part_up, Q_PM)
    gather(WQ, qs(WQ, ox, yb, c), Q_RP, dev(xh, ya, c))
    gather(WQ, part_down, SIB_Q + 4, d_sib)
    gather(WQ, part_up, SIB_Q + 5, d_sib)

    send(qs(DQ, 0, far, c), R1Q.at[0], R1_Q + 0, d_up)
    send(qs(DQ, 1, far, c), R1Q.at[1], R1_Q + 1, d_down)
    send(os(DO, 0, far, c), R1O.at[0], R1_O + 0, d_up)
    send(os(DO, 1, far, c), R1O.at[1], R1_O + 1, d_down)
    send(qs(DQ, 1, up, c), R2Q.at[0, 1], R2_Q + 1, d_up)
    send(qs(DQ, 0, down, c), R2Q.at[1, 0], R2_Q + 2, d_down)

    o_far = os(WO, xh, far, c)
    recv(os(WO, xh, far, c, 0, 32), O_RA)
    recv(os(WO, xh, far, c, 32, 32), O_RB)
    gather(WO, o_far, O_X2, d_x)
    gather(WO, o_far, SIB_O + 3, d_sib)
    for i, (yy, slot) in enumerate(((y, O_X0), (down, O_XP), (up, O_XM), (far, O_X2))):
        piece = os(WO, ox, yy, c)
        recv(piece, slot)
        gather(WO, piece, SIB_O + 4 + i, d_sib)
    far_own, far_part = qs(WQ, xh, far, c), qs(WQ, ox, far, c)
    recv(far_own, Q_RO)
    gather(WQ, far_own, SIB_Q + 6, d_sib)
    recv(far_part, Q_RP)
    gather(WQ, far_part, SIB_Q + 7, d_sib)

    loads[5].wait()
    for i in range(8):
        recv(mine_o, SIB_O + i)

    def grad_cols(n, carry):
        rhs = WO[pl.ds(2 * n, 2)].reshape(256, D)
        AGR[:, pl.ds(pl.multiple_of(n * 256, 256), 256)] = dot(G[b_slot], rhs, 1, 1).astype(BF)
        return carry

    lax.fori_loop(0, 4, grad_cols, 0)
    loads[4].wait()
    for i in range(8):
        recv(mine_q, SIB_Q + i)

    lane = lax.broadcasted_iota(jnp.int32, (SEQ, 128), 1)
    first_half = lane % 64 < 32
    low = lane < 64

    def rot(u):
        return jnp.where(first_half, pltpu.roll(u, 96, 1), pltpu.roll(u, 32, 1))

    def rope(u):
        return u * cos_ref[...] + rot(u) * sin_ref[...]

    def unrope(u):
        return u * cos_ref[...] - rot(u) * sin_ref[...]

    def qkv_tile(n):
        sl = pl.ds(pl.multiple_of(n * 256, 256), 256)
        return dot(N[...], WQ[:, :, sl].reshape(D, 256), 1, 0)

    def q_cols(n, carry):
        t = qkv_tile(n)
        for i in range(2):
            Q[2 * n + i] = rope(t[:, i * 128 : (i + 1) * 128]).astype(BF)
        return carry

    lax.fori_loop(0, 4, q_cols, 0)
    for n, dst in ((4, KD), (5, VD)):
        t = qkv_tile(n)
        for i in range(2):
            u = t[:, i * 128 : (i + 1) * 128]
            if n == 4:
                u = rope(u)
            r = pltpu.roll(u, 64, 1)
            dst[2 * i] = jnp.where(low, u, r).astype(BF)
            dst[2 * i + 1] = jnp.where(low, r, u).astype(BF)

    causal = lax.broadcasted_iota(jnp.int32, (SEQ, SEQ), 0) <= lax.broadcasted_iota(
        jnp.int32, (SEQ, SEQ), 1
    )

    def one_kv(kv, carry):
        kd, vd = KD[kv], VD[kv]
        DKD[...] = jnp.zeros_like(DKD)
        DVD[...] = jnp.zeros_like(DVD)

        def pair(i, carry):
            t = kv * 2 + i
            q2 = Q[t]
            g2 = AGR[:, pl.ds(pl.multiple_of(t * 128, 128), 128)]
            dqs = []
            for keep in (low, jnp.logical_not(low)):
                qm = jnp.where(keep, q2, jnp.zeros_like(q2))
                gm = jnp.where(keep, g2, jnp.zeros_like(g2))
                e = jnp.where(causal, jnp.exp(dot(kd, qm, 1, 1) * SCALE), 0.0)
                probs = e * (1.0 / jnp.sum(e, axis=0, keepdims=True))
                DVD[...] += dot(probs.astype(BF), gm, 1, 0)
                dp = dot(vd, gm, 1, 1)
                delta = jnp.sum(probs * dp, axis=0, keepdims=True)
                ds = (probs * (dp - delta) * SCALE).astype(BF)
                DKD[...] += dot(ds, qm, 1, 0)
                dqs.append(dot(ds, kd, 0, 0))
            dq = jnp.where(low, dqs[0], dqs[1])
            GP[:, pl.ds(pl.multiple_of(t * 128, 128), 128)] = unrope(dq).astype(BF)
            return carry

        lax.fori_loop(0, 2, pair, 0)
        dk = DKD[...]
        dk = unrope(dk + pltpu.roll(dk, 64, 1))
        dv = DVD[...]
        dv = dv + pltpu.roll(dv, 64, 1)
        even = kv % 2 == 0
        keep = jnp.logical_xor(low, jnp.logical_not(even))
        for base, val in ((QW, dk), (QW + 256, dv)):
            sl = pl.ds(pl.multiple_of(base + (kv // 2) * 128, 128), 128)
            GP[:, sl] = jnp.where(keep, val.astype(BF), GP[:, sl])
        return carry

    GP[:, QW:] = jnp.zeros((SEQ, 512), BF)
    lax.fori_loop(0, 2, one_kv, 0)

    def add_into(dst, other):
        dst[...] = (dst[...].astype(F32) + other.astype(F32)).astype(BF)

    recv(R1Q.at[0], R1_Q + 0)
    add_into(qs(DQ, 0, up, c), R1Q[0])
    recv(R1Q.at[1], R1_Q + 1)
    add_into(qs(DQ, 1, down, c), R1Q[1])
    send(qs(DQ, 0, up, c), R2Q.at[0, 0], R2_Q + 0, d_up)
    send(qs(DQ, 1, down, c), R2Q.at[1, 1], R2_Q + 3, d_down)
    send(os(DO, 1, up, c), R2O.at[0, 1], R2_O + 1, d_up)
    send(os(DO, 0, down, c), R2O.at[1, 0], R2_O + 2, d_down)

    lax.fori_loop(2, 4, one_kv, 0)

    recv(R1O.at[0], R1_O + 0)
    add_into(os(DO, 0, up, c), R1O[0])
    recv(R1O.at[1], R1_O + 1)
    add_into(os(DO, 1, down, c), R1O[1])
    send(os(DO, 0, up, c), R2O.at[0, 0], R2_O + 0, d_up)
    send(os(DO, 1, down, c), R2O.at[1, 1], R2_O + 3, d_down)

    DOT[...] = jnp.zeros_like(DOT)

    def normed_cols(j, carry):
        sl = pl.ds(pl.multiple_of(j * 256, 256), 256)
        u = dot(GP[...], WQ[j], 1, 1) * gain_ref[:, sl]
        U[:, sl] = u
        ux = u * X[b_slot, :, sl].astype(F32)
        DOT[...] += ux[:, :128] + ux[:, 128:]
        return carry

    lax.fori_loop(0, CHIPS, normed_cols, 0)

    def finish(r, carry):
        sl = pl.ds(pl.multiple_of(r * 16, 16), 16)
        inv = INV[sl, :][:, :1]
        mean = jnp.sum(DOT[sl, :], axis=-1, keepdims=True) * (1.0 / D)
        wide = X[b_slot, sl, :].astype(F32)
        res = G[b_slot, sl, :].astype(F32) + inv * U[sl, :] - wide * (inv * inv * inv * mean)
        OUT[sl, :] = res.astype(BF)
        return carry

    for k in range(3):
        lax.fori_loop(8 * k, 8 * k + 8, finish, 0)
        rows = pl.ds(128 * k, 128)
        send(OUT.at[rows], prev_hbm.at[rows], PERM + k, d_prev)

    for i in range(4):
        recv(R2Q.at[i // 2, i % 2], R2_Q + i)

    def total(D_, slicer, R2, xx):
        return (
            slicer(D_, xx, y, c)[...].astype(F32) + R2[0, xx].astype(F32) + R2[1, xx].astype(F32)
        )

    theirs = qs(DQ, ox, y, c)
    theirs[...] = total(DQ, qs, R2Q, ox).astype(BF)
    gq_ref[...] = total(DQ, qs, R2Q, xh)
    send(theirs, RXQ, RX_Q, d_x)
    for i in range(4):
        recv(R2O.at[i // 2, i % 2], R2_O + i)
    theirs = os(DO, ox, y, c)
    theirs[...] = total(DO, os, R2O, ox).astype(BF)
    go_ref[...] = total(DO, os, R2O, xh)
    send(theirs, RXO, RX_O, d_x)
    recv(RXQ, RX_Q)
    gq_ref[...] += RXQ[...].astype(F32)
    recv(RXO, RX_O)
    go_ref[...] += RXO[...].astype(F32)
    for k in range(3):
        recv(prev_hbm.at[pl.ds(128 * k, 128)], PERM + k)
    for cp in started:
        cp.wait_send()


def local(x, g, a, p, wq, wo, gain, b, w):
    cos, sin = rope_tables()
    any_ = pl.BlockSpec(memory_space=pl.ANY)
    vm = pl.BlockSpec(memory_space=pltpu.VMEM)
    sm = pl.BlockSpec(memory_space=pltpu.SMEM)
    V = pltpu.VMEM
    prev, gq, go = pl.pallas_call(
        kernel,
        name="step",
        out_shape=(
            jax.ShapeDtypeStruct((SEQ, D), BF),
            jax.ShapeDtypeStruct((128, QKVW), F32),
            jax.ShapeDtypeStruct((64, D), F32),
        ),
        in_specs=[any_] * 6 + [vm, sm, sm, vm, vm],
        out_specs=(any_, vm, vm),
        scratch_shapes=[
            V((2, SEQ, D), BF), V((2, SEQ, D), BF), V((2, SEQ, QW), BF), V((2, SEQ, QKVW), BF),
            V((CHIPS, 256, QKVW), BF), V((CHIPS, 128, D), BF),
            V((CHIPS, 256, QKVW), BF), V((CHIPS, 128, D), BF),
            V((CHIPS, 128, QKVW), BF), V((CHIPS, 64, D), BF),
            V((2, 128, QKVW), BF), V((2, 64, D), BF),
            V((2, 2, 128, QKVW), BF), V((2, 2, 64, D), BF),
            V((128, QKVW), BF), V((64, D), BF),
            V((SEQ, D), BF), V((SEQ, 128), F32), V((8, SEQ, 128), BF),
            V((KV_HEADS, SEQ, 128), BF), V((KV_HEADS, SEQ, 128), BF),
            V((SEQ, QW), BF), V((SEQ, QKVW), BF), V((SEQ, 128), F32), V((SEQ, 128), F32),
            V((SEQ, D), F32), V((SEQ, 128), F32), V((SEQ, D), BF),
            pltpu.SemaphoreType.DMA((6,)),
            pltpu.SemaphoreType.DMA((N_SEM,)),
            pltpu.SemaphoreType.DMA((N_SEM,)),
        ],
        compiler_params=pltpu.CompilerParams(
            collective_id=0, has_side_effects=True, vmem_limit_bytes=67043328
        ),
    )(
        x[0], g[0], a[0], p[0], wq[0], wo[0], gain, b, w, jnp.asarray(cos), jnp.asarray(sin)
    )
    return prev[None], gq[None], go[None]


def solution(mesh):
    row = P("section", None, "fsdp", None)
    out = P("section", "fsdp", None)
    return jax.shard_map(
        local,
        mesh=mesh,
        in_specs=(row, row, row, row, out, out, P("section", None), P("section"), P("section")),
        out_specs=(out, out, out),
        check_vma=False,
    )
```

time: 282 us -> 137 us (0.49)
  waiting for transfers between devices: 157 us -> 0 us
  Pallas kernels: 0 us -> 130 us
  matrix products: 76.1 us -> 0 us
  between operations: 17.3 us -> 1.95 us
  other arithmetic: 15.3 us -> 0 us
  local copies, waits for them, and re-layouts: 12.9 us -> 4.51 us
    pallas_call x0 -> x1, Pallas kernels: none -> 130 us  [local(): pl.pallas_call(kernel, name='step', out_shape=(jax.ShapeDtypeStruct((SEQ,...]
    all_gather x2 -> x0, waiting for transfers between devices: 123 us -> none  [the longest x1 79.5 us: local(): whole_qkv = lax.all_gather(qkv_shard, FSDP, axis=0, tiled=True)]
    dot_general x10 -> x0, matrix products: 76.1 us -> none  [the longest x5 52.3 us: contract(): jnp.einsum(pattern, first_operand, second_operand, preferred_element_type...]
    ppermute x1 -> x0, waiting for transfers between devices: 32.1 us -> none  [passed_along(): lax.ppermute(array, axis, [(i, (i + by) % size) for i in range(size)])]
    slice x6 -> x0, local copies, waits for them, and re-layouts: 5.8 us -> none  [the longest x2 3.16 us: attention_back(): qkv_rows[:, :q_width].reshape(tokens_here, HEADS, HEAD_DIM)]
    convert_element_type x4 -> x0, other arithmetic: 4.16 us -> none  [the longest x1 2.02 us: finish_grad(): return result.astype(jnp.bfloat16)]
    reduce_sum x2 -> x0, other arithmetic: 3.63 us -> none  [normalize(): jnp.mean(widened * widened, axis=-1, keepdims=True) + rms_eps]
  transfers between devices with their start and end apart: 6 -> 0, of which waited for: 3 -> 0; matrix products, arithmetic and copies ran while one was open for 36% -> 0% of each run, Pallas kernels for 0% -> 0%
where the time goes in v1:
time: 137 us
  Pallas kernels  130 us (95%)
  local copies, waits for them, and re-layouts  4.51 us (3%)
  between operations  1.95 us (1%)
    pallas_call x1, Pallas kernels, local(): pl.pallas_call(kernel, name='step', out_shape=(jax.ShapeDtypeStruct((SEQ,...  130 us
    unnamed x7, local copies, waits for them, and re-layouts  4.51 us

profile of v1, /device:TPU:97, one launch (start us, length us, event | category | flops | bytes accessed | tf_op | source)
XLA Modules:
  0.0 136.6 jit_solution(2474637877690481138)
XLA Ops:
  1.9 130.1 %step.1 = (bf16[384,2048]{1,0:T(8,128)(2,1)}, f32[128,1536]{1,0:T(8,128)}, f32[64,2048]{1,0:T(8,128)}) custom-call(bf16[2,384,2048]{2,1,0:T(8,128)(2,1)} %bitcast.9, bf16[2,384,2048]{2,1,0:T(8,128)(2,1)} %bitcast.10, bf16[2,384,1024]{2,1,0:T(8,128)(2,1)} %bitcast.12, bf16[2,384,1536]{2,1,0:T(8,128)(2,1)} %bitcast.11, bf16[128,1536]{1,0:T(8,128)(2,1)} %bitcast.16, ...), custom_call_target="tpu_custom_call" | custom-call | tf_op jit(solution)/shard_map/step/pallas_call | solution.py:406
  132.1 0.0 copy-start
  132.1 0.0 copy-start.1
  132.1 2.8 %copy.19 = bf16[1,384,2048]{2,1,0:T(8,128)(2,1)} copy(bf16[1,384,2048]{2,1,0:T(8,128)(2,1)} %bitcast.13) | data formatting | bytes 3145728
  134.9 0.0 copy-done
  134.9 0.9 copy.20
  135.8 0.0 copy-done.1
  135.8 0.8 copy.21
Async XLA Ops:
  132.1 2.9 %copy-start = (f32[128,1536]{1,0:T(8,128)S(1)}, f32[128,1536]{1,0:T(8,128)}, u32[]{:S(2)}) copy-start(f32[128,1536]{1,0:T(8,128)} %get-tuple-element.7) | copy-start | bytes 2359300
  132.1 3.7 %copy-start.1 = (f32[64,2048]{1,0:T(8,128)S(1)}, f32[64,2048]{1,0:T(8,128)}, u32[]{:S(2)}) copy-start(f32[64,2048]{1,0:T(8,128)} %get-tuple-element.8) | copy-start | bytes 1572868

commit v2 on v1

v2 whole, which is shorter than its diff:
```python
import functools

import jax
import jax.numpy as jnp
import numpy as np
from jax import lax
from jax.experimental import pallas as pl
from jax.experimental.pallas import tpu as pltpu
from jax.sharding import PartitionSpec as P

D = 2048
HEAD_DIM = 64
HEADS = 16
KV_HEADS = 4
SEQ = 384
QW = 1024
QKVW = 1536
CHIPS = 8
EPS = 1e-05
SCALE = HEAD_DIM ** (-0.5)
BF = jnp.bfloat16
F32 = jnp.float32
MESH = pl.DeviceIdType.MESH

Q_X, Q_YP, Q_YM, Q_PP, Q_PM, Q_RO, Q_RP = range(7)
O_YP, O_YM, O_X0, O_XP, O_XM, O_X2, O_RA, O_RB = range(7, 15)
SIB_Q = 15
SIB_O = 23
RS_SIB_Q, RS_SIB_O = 31, 32
R1_Q, R1_O = 33, 35
R2_Q, R2_O = 37, 41
RX_Q, RX_O = 45, 46
PERM = 47
N_SEM = 50


def rope_tables():
    half = HEAD_DIM // 2
    freq = 500000.0 ** (-2.0 * np.arange(half) / HEAD_DIM)
    ang = np.arange(SEQ)[:, None] * freq[None, :]
    cos = np.tile(np.cos(ang), (1, 4)).astype(np.float32)
    sin = np.tile(np.sin(ang), (1, 4)).astype(np.float32)
    sign = np.where(np.arange(128) % 64 < 32, -1.0, 1.0).astype(np.float32)
    return cos, sin * sign[None, :]


def dot(a, b, ca, cb):
    return lax.dot_general(a, b, (((ca,), (cb,)), ((), ())), preferred_element_type=F32)


def kernel(
    x_hbm, g_hbm, a_hbm, p_hbm, wq_hbm, wo_hbm, gain_ref, b_ref, w_ref, cos_ref, sin_ref,
    prev_hbm, gq_ref, go_ref,
    X, G, A, PG, WQ, WO, DQ, DO, SQ, SO, R1Q, R1O, R2Q, R2O, RXQ, RXO,
    N, INV, QKV, QS, GS, KD, VD, GP, DK, DV, U, DOT, OUT,
    lsem, ssem, rsem,
):
    s = lax.axis_index("section")
    f = lax.axis_index("fsdp")
    xh, y, c = f // 8, (f // 2) % 4, f % 2
    up, down, far = (y + 1) % 4, (y + 3) % 4, (y + 2) % 4
    oc, ox = 1 - c, 1 - xh
    n_sec = lax.axis_size("section")

    def dev(xx, yy, cc):
        return (s, xx * 8 + yy * 2 + cc)

    d_up, d_down, d_x, d_sib = dev(xh, up, c), dev(xh, down, c), dev(ox, y, c), dev(xh, y, oc)
    d_prev, d_next = (lax.rem(s + n_sec - 1, n_sec), f), (lax.rem(s + 1, n_sec), f)

    def qs(ref, xx, yy, cc):
        return ref.at[xx * 4 + yy, pl.ds(pl.multiple_of(cc * 128, 128), 128), :]

    def os(ref, xx, yy, cc, lo=0, n=64):
        return ref.at[xx * 4 + yy, pl.ds(pl.multiple_of(cc * 64 + lo, 32), n), :]

    started = []
    scope = []

    def phase(name):
        if scope:
            scope.pop().__exit__(None, None, None)
        if name:
            scope.append(jax.named_scope(name))
            scope[-1].__enter__()

    def rcopy(src, dst, slot, device):
        return pltpu.make_async_remote_copy(
            src_ref=src, dst_ref=dst, send_sem=ssem.at[slot], recv_sem=rsem.at[slot],
            device_id=device, device_id_type=MESH,
        )

    def send(src, dst, slot, device):
        cp = rcopy(src, dst, slot, device)
        cp.start()
        started.append(cp)

    def recv(dst, slot):
        rcopy(dst, dst, slot, d_sib).wait_recv()

    def gather(ref, shard, slot, device, src=None):
        send(shard if src is None else src, shard, slot, device)

    phase("entry")
    barrier = pltpu.get_barrier_semaphore()
    for d in (d_up, d_down, d_x, d_sib, d_prev, d_next):
        pl.semaphore_signal(barrier, inc=1, device_id=d, device_id_type=MESH)
    loads = [
        pltpu.make_async_copy(g_hbm, G, lsem.at[0]),
        pltpu.make_async_copy(a_hbm, A, lsem.at[1]),
        pltpu.make_async_copy(x_hbm, X, lsem.at[2]),
        pltpu.make_async_copy(p_hbm, PG, lsem.at[3]),
        pltpu.make_async_copy(wq_hbm, qs(WQ, xh, y, c), lsem.at[4]),
        pltpu.make_async_copy(wo_hbm, os(WO, xh, y, c), lsem.at[5]),
    ]
    for cp in (loads[4], loads[5], loads[0], loads[1], loads[2], loads[3]):
        cp.start()
    pl.semaphore_wait(barrier, 6)

    phase("own_out")
    mine_q, mine_o = qs(WQ, xh, y, c), os(WO, xh, y, c)
    gather(WQ, mine_q, Q_X, d_x, wq_hbm)
    gather(WQ, mine_q, Q_YP, d_up, wq_hbm)
    gather(WQ, mine_q, Q_YM, d_down, wq_hbm)
    gather(WO, mine_o, O_YP, d_up, wo_hbm)
    gather(WO, mine_o, O_YM, d_down, wo_hbm)
    gather(WO, mine_o, O_X0, d_x, wo_hbm)
    gather(WQ, mine_q, SIB_Q + 0, d_sib, wq_hbm)
    gather(WO, mine_o, SIB_O + 0, d_sib, wo_hbm)

    b_slot, w_slot = b_ref[0], w_ref[0]

    phase("dw_out")
    loads[0].wait()
    loads[1].wait()

    def out_part(j, carry):
        lhs = A[w_slot, :, pl.ds(pl.multiple_of(j * 256, 256), 256)]
        part = dot(lhs, G[w_slot], 0, 0).astype(BF)
        DO[pl.ds(2 * j, 2)] = part.reshape(2, 128, D)
        return carry

    lax.fori_loop(0, 4, out_part, 0)
    send(DO.at[:, pl.ds(pl.multiple_of(oc * 64, 64), 64), :], SO, RS_SIB_O, d_sib)
    phase("norm_w")
    loads[2].wait()
    loads[3].wait()

    def norm(slot):
        def rows(r, carry):
            sl = pl.ds(pl.multiple_of(r * 16, 16), 16)
            wide = X[slot, sl, :].astype(F32)
            inv = lax.rsqrt(jnp.mean(wide * wide, axis=-1, keepdims=True) + EPS)
            INV[sl, :] = jnp.broadcast_to(inv, (16, 128))
            N[sl, :] = (wide * inv * gain_ref[...]).astype(BF)
            return carry

        lax.fori_loop(0, SEQ // 16, rows, 0, unroll=4)

    norm(w_slot)

    phase("dw_qkv")

    def qkv_part(j, carry):
        lhs = N[:, pl.ds(pl.multiple_of(j * 256, 256), 256)]
        DQ[j] = dot(lhs, PG[w_slot], 0, 0).astype(BF)
        return carry

    lax.fori_loop(0, CHIPS, qkv_part, 0)
    send(DQ.at[:, pl.ds(pl.multiple_of(oc * 128, 128), 128), :], SQ, RS_SIB_Q, d_sib)
    phase("norm_b")
    norm(b_slot)

    lane = lax.broadcasted_iota(jnp.int32, (128, 128), 1)
    first_half = lane % 64 < 32
    low = lane < 64

    def acc_qkv(xx, yy, first=False):
        j = xx * 4 + yy
        part = dot(N[:, pl.ds(pl.multiple_of(j * 256, 256), 256)], WQ[j], 1, 0)
        QKV[...] = part if first else QKV[...] + part

    def stack(ref, qb, kv, i, tile):
        zero = jnp.zeros_like(tile)
        ref[qb, kv, pl.ds(pl.multiple_of(i * 256, 256), 128)] = jnp.where(low, tile, zero)
        ref[qb, kv, pl.ds(pl.multiple_of(i * 256 + 128, 128), 128)] = jnp.where(low, zero, tile)

    def attn_grad(xx, yy):
        j = xx * 4 + yy
        tile = dot(G[b_slot], WO[j], 1, 1).astype(BF)
        for qb in range(3):
            stack(GS, qb, j // 2, j % 2, tile[qb * 128 : (qb + 1) * 128])

    def pair_sum_o(j, carry):
        so = pl.ds(pl.multiple_of(c * 64, 64), 64)
        DO[j, so, :] = (DO[j, so, :].astype(F32) + SO[j].astype(F32)).astype(BF)
        return carry

    def pair_sum_q(j, carry):
        sq = pl.ds(pl.multiple_of(c * 128, 128), 128)
        DQ[j, sq, :] = (DQ[j, sq, :].astype(F32) + SQ[j].astype(F32)).astype(BF)
        return carry

    sgn = 1 - 2 * xh
    ya, yb = (y + 4 - sgn) % 4, (y + 4 + sgn) % 4
    phase("fwd_xq")
    part_q = qs(WQ, ox, y, c)
    recv(part_q, Q_X)
    gather(WQ, part_q, Q_PP, d_up)
    gather(WQ, part_q, Q_PM, d_down)
    gather(WQ, part_q, SIB_Q + 1, d_sib)
    phase("fwd_yq")
    from_down, from_up = qs(WQ, xh, down, c), qs(WQ, xh, up, c)
    recv(from_down, Q_YP)
    recv(from_up, Q_YM)
    gather(WQ, from_down, SIB_Q + 2, d_sib)
    gather(WQ, from_up, SIB_Q + 3, d_sib)
    phase("sum_o")
    recv(SO, RS_SIB_O)
    lax.fori_loop(0, CHIPS, pair_sum_o, 0)
    phase("qkv_0")
    loads[4].wait()
    recv(mine_q, SIB_Q + 0)
    acc_qkv(xh, y, first=True)
    recv(mine_q, SIB_Q + 1)
    acc_qkv(ox, y)
    phase("fwd_yo")
    o_down, o_up = os(WO, xh, down, c), os(WO, xh, up, c)
    recv(o_down, O_YP)
    recv(o_up, O_YM)
    gather(WO, os(WO, xh, down, c, 0, 32), O_RA, d_up)
    gather(WO, os(WO, xh, up, c, 32, 32), O_RB, d_down)
    gather(WO, o_down, O_XP, d_x)
    gather(WO, o_up, O_XM, d_x)
    gather(WQ, qs(WQ, xh, ya, c), Q_RO, dev(xh, yb, c))
    gather(WO, o_down, SIB_O + 1, d_sib)
    gather(WO, o_up, SIB_O + 2, d_sib)
    o_part = os(WO, ox, y, c)
    recv(o_part, O_X0)
    gather(WO, o_part, SIB_O + 4, d_sib)
    phase("sum_q")
    recv(SQ, RS_SIB_Q)
    lax.fori_loop(0, CHIPS, pair_sum_q, 0)
    phase("qkv_1")
    recv(mine_q, SIB_Q + 2)
    acc_qkv(xh, down)
    recv(mine_q, SIB_Q + 3)
    acc_qkv(xh, up)
    phase("ag_0")
    loads[5].wait()
    recv(mine_o, SIB_O + 0)
    attn_grad(xh, y)
    recv(mine_o, SIB_O + 1)
    attn_grad(xh, down)

    phase("fwd_yp")
    part_down, part_up = qs(WQ, ox, down, c), qs(WQ, ox, up, c)
    recv(part_down, Q_PP)
    recv(part_up, Q_PM)
    gather(WQ, qs(WQ, ox, yb, c), Q_RP, dev(xh, ya, c))
    gather(WQ, part_down, SIB_Q + 4, d_sib)
    gather(WQ, part_up, SIB_Q + 5, d_sib)

    send(qs(DQ, 0, far, c), R1Q.at[0], R1_Q + 0, d_up)
    send(qs(DQ, 1, far, c), R1Q.at[1], R1_Q + 1, d_down)
    send(os(DO, 0, far, c), R1O.at[0], R1_O + 0, d_up)
    send(os(DO, 1, far, c), R1O.at[1], R1_O + 1, d_down)
    send(qs(DQ, 1, up, c), R2Q.at[0, 1], R2_Q + 1, d_up)
    send(qs(DQ, 0, down, c), R2Q.at[1, 0], R2_Q + 2, d_down)

    phase("fwd_ofar")
    o_far = os(WO, xh, far, c)
    recv(os(WO, xh, far, c, 0, 32), O_RA)
    recv(os(WO, xh, far, c, 32, 32), O_RB)
    gather(WO, o_far, O_X2, d_x)
    gather(WO, o_far, SIB_O + 3, d_sib)

    def pass_o(yy, slot, i):
        piece = os(WO, ox, yy, c)
        recv(piece, slot)
        gather(WO, piece, SIB_O + i, d_sib)

    pass_o(down, O_XP, 5)
    phase("ag_1")
    recv(mine_o, SIB_O + 2)
    attn_grad(xh, up)
    recv(mine_o, SIB_O + 4)
    attn_grad(ox, y)
    phase("fwd_xo")
    pass_o(up, O_XM, 6)
    phase("qkv_2")
    recv(mine_q, SIB_Q + 4)
    acc_qkv(ox, down)
    recv(mine_q, SIB_Q + 5)
    acc_qkv(ox, up)
    phase("ag_2")
    recv(mine_o, SIB_O + 5)
    attn_grad(ox, down)
    recv(mine_o, SIB_O + 3)
    attn_grad(xh, far)
    phase("fwd_qfar")
    far_own, far_part = qs(WQ, xh, far, c), qs(WQ, ox, far, c)
    recv(far_own, Q_RO)
    gather(WQ, far_own, SIB_Q + 6, d_sib)
    pass_o(far, O_X2, 7)
    recv(far_part, Q_RP)
    gather(WQ, far_part, SIB_Q + 7, d_sib)
    phase("ag_3")
    recv(mine_o, SIB_O + 6)
    attn_grad(ox, up)
    recv(mine_o, SIB_O + 7)
    attn_grad(ox, far)
    phase("qkv_3")
    recv(mine_q, SIB_Q + 6)
    acc_qkv(xh, far)
    recv(mine_q, SIB_Q + 7)
    acc_qkv(ox, far)

    phase("rope")

    def rot(u):
        return jnp.where(first_half, pltpu.roll(u, 96, 1), pltpu.roll(u, 32, 1))

    def rope(u, rows):
        return u * cos_ref[rows, :] + rot(u) * sin_ref[rows, :]

    def unrope(u, rows):
        return u * cos_ref[rows, :] - rot(u) * sin_ref[rows, :]

    for qb in range(3):
        rows = pl.ds(qb * 128, 128)

        def q_tile(t, carry):
            u = QKV[rows, pl.ds(pl.multiple_of(t * 128, 128), 128)]
            stack(QS, qb, t // 2, t % 2, rope(u, rows).astype(BF))
            return carry

        lax.fori_loop(0, 8, q_tile, 0, unroll=2)
        for base, dst in ((QW, KD), (QW + 256, VD)):
            for i in range(2):
                u = QKV[rows, base + i * 128 : base + (i + 1) * 128]
                if dst is KD:
                    u = rope(u, rows)
                r = pltpu.roll(u, 64, 1)
                dst[2 * i, rows, :] = jnp.where(low, u, r).astype(BF)
                dst[2 * i + 1, rows, :] = jnp.where(low, r, u).astype(BF)

    diag = lax.broadcasted_iota(jnp.int32, (128, 512), 0) <= (
        lax.broadcasted_iota(jnp.int32, (128, 512), 1) % 128
    )
    exp_scale = SCALE * 1.4426950408889634

    def attend(qb):
        keys = 128 * (qb + 1)
        rows = pl.ds(qb * 128, 128)

        def one_kv(kv, carry):
            kd, vd = KD[kv, :keys], VD[kv, :keys]
            q4, g4 = QS[qb, kv], GS[qb, kv]
            e = jnp.exp2(dot(kd, q4, 1, 1) * exp_scale)
            last = jnp.where(diag, e[keys - 128 :], 0.0)
            e = last if qb == 0 else jnp.concatenate([e[: keys - 128], last], axis=0)
            probs = e * (1.0 / jnp.sum(e, axis=0, keepdims=True))
            dv = dot(probs.astype(BF), g4, 1, 0)
            dp = dot(vd, g4, 1, 1)
            delta = jnp.sum(probs * dp, axis=0, keepdims=True)
            ds = (probs * (dp - delta)).astype(BF)
            dk = dot(ds, q4, 1, 0) * SCALE
            dq = dot(ds, kd, 0, 0) * SCALE
            if qb == 2:
                DK[kv], DV[kv] = dk, dv
            else:
                DK[kv, :keys] += dk
                DV[kv, :keys] += dv
            for i in range(2):
                tile = jnp.where(low, dq[256 * i : 256 * i + 128], dq[256 * i + 128 : 256 * i + 256])
                sl = pl.ds(pl.multiple_of((2 * kv + i) * 128, 128), 128)
                GP[:, sl] = unrope(tile, rows).astype(BF)
            return carry

        lax.fori_loop(0, KV_HEADS, one_kv, 0)
        for i in range(2):
            for base, ref in ((QW, DK), (QW + 256, DV)):
                halves = []
                for kv in (2 * i, 2 * i + 1):
                    t = ref[kv, rows]
                    halves.append(t + pltpu.roll(t, 64, 1))
                tile = jnp.where(low, halves[0], halves[1])
                if ref is DK:
                    tile = unrope(tile, rows)
                GP[:, base + i * 128 : base + (i + 1) * 128] = tile.astype(BF)

    def input_grad(qb):
        rows = pl.ds(qb * 128, 128)
        DOT[...] = jnp.zeros_like(DOT)

        def normed_cols(j, carry):
            sl = pl.ds(pl.multiple_of(j * 256, 256), 256)
            u = dot(GP[...], WQ[j], 1, 1) * gain_ref[:, sl]
            U[:, sl] = u
            ux = u * X[b_slot, rows, sl].astype(F32)
            DOT[...] += ux[:, :128] + ux[:, 128:]
            return carry

        lax.fori_loop(0, CHIPS, normed_cols, 0, unroll=2)
        inv = INV[rows, :]
        mean = jnp.sum(DOT[...], axis=-1, keepdims=True) * (1.0 / D)
        DOT[...] = inv * inv * inv * mean

        def finish(j, carry):
            for r in range(4):
                part = pl.ds(32 * r, 32)
                here = pl.ds(qb * 128 + 32 * r, 32)
                sl = pl.ds(pl.multiple_of(j * 128, 128), 128)
                res = (
                    G[b_slot, here, sl].astype(F32)
                    + INV[here, :] * U[part, sl]
                    - X[b_slot, here, sl].astype(F32) * DOT[part, :]
                )
                OUT[here, sl] = res.astype(BF)
            return carry

        lax.fori_loop(0, 16, finish, 0, unroll=2)
        send(OUT.at[rows], prev_hbm.at[rows], PERM + qb, d_prev)

    def add_into(dst, other):
        dst[...] = (dst[...].astype(F32) + other.astype(F32)).astype(BF)

    phase("attn_2")
    attend(2)
    phase("ig_2")
    input_grad(2)

    phase("rs_relay_q")
    recv(R1Q.at[0], R1_Q + 0)
    add_into(qs(DQ, 0, up, c), R1Q[0])
    recv(R1Q.at[1], R1_Q + 1)
    add_into(qs(DQ, 1, down, c), R1Q[1])
    send(qs(DQ, 0, up, c), R2Q.at[0, 0], R2_Q + 0, d_up)
    send(qs(DQ, 1, down, c), R2Q.at[1, 1], R2_Q + 3, d_down)
    send(os(DO, 1, up, c), R2O.at[0, 1], R2_O + 1, d_up)
    send(os(DO, 0, down, c), R2O.at[1, 0], R2_O + 2, d_down)
    phase("attn_1")
    attend(1)
    phase("ig_1")
    input_grad(1)
    phase("rs_relay_o")
    recv(R1O.at[0], R1_O + 0)
    add_into(os(DO, 0, up, c), R1O[0])
    recv(R1O.at[1], R1_O + 1)
    add_into(os(DO, 1, down, c), R1O[1])
    send(os(DO, 0, up, c), R2O.at[0, 0], R2_O + 0, d_up)
    send(os(DO, 1, down, c), R2O.at[1, 1], R2_O + 3, d_down)
    phase("attn_0")
    attend(0)
    phase("ig_0")
    input_grad(0)

    phase("rs_wait_q")
    for i in range(4):
        recv(R2Q.at[i // 2, i % 2], R2_Q + i)

    phase("rs_tot_q")
    def total(D_, slicer, R2, xx):
        return (
            slicer(D_, xx, y, c)[...].astype(F32) + R2[0, xx].astype(F32) + R2[1, xx].astype(F32)
        )

    theirs = qs(DQ, ox, y, c)
    theirs[...] = total(DQ, qs, R2Q, ox).astype(BF)
    gq_ref[...] = total(DQ, qs, R2Q, xh)
    send(theirs, RXQ, RX_Q, d_x)
    phase("rs_wait_o")
    for i in range(4):
        recv(R2O.at[i // 2, i % 2], R2_O + i)
    theirs = os(DO, ox, y, c)
    theirs[...] = total(DO, os, R2O, ox).astype(BF)
    go_ref[...] = total(DO, os, R2O, xh)
    send(theirs, RXO, RX_O, d_x)
    phase("rs_x_wait")
    recv(RXQ, RX_Q)
    gq_ref[...] += RXQ[...].astype(F32)
    recv(RXO, RX_O)
    go_ref[...] += RXO[...].astype(F32)
    phase("perm_wait")
    for k in range(3):
        recv(prev_hbm.at[pl.ds(128 * k, 128)], PERM + k)
    phase("send_wait")
    for cp in started:
        cp.wait_send()
    phase(None)


def local(x, g, a, p, wq, wo, gain, b, w):
    cos, sin = rope_tables()
    any_ = pl.BlockSpec(memory_space=pl.ANY)
    vm = pl.BlockSpec(memory_space=pltpu.VMEM)
    sm = pl.BlockSpec(memory_space=pltpu.SMEM)
    V = pltpu.VMEM
    prev, gq, go = pl.pallas_call(
        kernel,
        name="step",
        out_shape=(
            jax.ShapeDtypeStruct((SEQ, D), BF),
            jax.ShapeDtypeStruct((128, QKVW), F32),
            jax.ShapeDtypeStruct((64, D), F32),
        ),
        in_specs=[any_] * 6 + [vm, sm, sm, vm, vm],
        out_specs=(any_, vm, vm),
        scratch_shapes=[
            V((2, SEQ, D), BF), V((2, SEQ, D), BF), V((2, SEQ, QW), BF), V((2, SEQ, QKVW), BF),
            V((CHIPS, 256, QKVW), BF), V((CHIPS, 128, D), BF),
            V((CHIPS, 256, QKVW), BF), V((CHIPS, 128, D), BF),
            V((CHIPS, 128, QKVW), BF), V((CHIPS, 64, D), BF),
            V((2, 128, QKVW), BF), V((2, 64, D), BF),
            V((2, 2, 128, QKVW), BF), V((2, 2, 64, D), BF),
            V((128, QKVW), BF), V((64, D), BF),
            V((SEQ, D), BF), V((SEQ, 128), F32), V((SEQ, QKVW), F32),
            V((3, KV_HEADS, 512, 128), BF), V((3, KV_HEADS, 512, 128), BF),
            V((KV_HEADS, SEQ, 128), BF), V((KV_HEADS, SEQ, 128), BF),
            V((128, QKVW), BF), V((KV_HEADS, SEQ, 128), F32), V((KV_HEADS, SEQ, 128), F32),
            V((128, D), F32), V((128, 128), F32), V((SEQ, D), BF),
            pltpu.SemaphoreType.DMA((6,)),
            pltpu.SemaphoreType.DMA((N_SEM,)),
            pltpu.SemaphoreType.DMA((N_SEM,)),
        ],
        compiler_params=pltpu.CompilerParams(
            collective_id=0, has_side_effects=True, vmem_limit_bytes=67043328
        ),
    )(
        x[0], g[0], a[0], p[0], wq[0], wo[0], gain, b, w, jnp.asarray(cos), jnp.asarray(sin)
    )
    return prev[None], gq[None], go[None]


def solution(mesh):
    row = P("section", None, "fsdp", None)
    out = P("section", "fsdp", None)
    return jax.shard_map(
        local,
        mesh=mesh,
        in_specs=(row, row, row, row, out, out, P("section", None), P("section"), P("section")),
        out_specs=(out, out, out),
        check_vma=False,
    )
```

time: 137 us -> 117 us (0.85)
  Pallas kernels: 130 us -> 110 us
    pallas_call x1, Pallas kernels: 130 us -> 110 us  [local(): pl.pallas_call(kernel, name='step', out_shape=(jax.ShapeDtypeStruct((SEQ,...]
where the time goes in v2:
time: 117 us
  Pallas kernels  110 us (94%)
  local copies, waits for them, and re-layouts  4.51 us (4%)
  between operations  1.95 us (2%)
    pallas_call x1, Pallas kernels, local(): pl.pallas_call(kernel, name='step', out_shape=(jax.ShapeDtypeStruct((SEQ,...  110 us
    unnamed x7, local copies, waits for them, and re-layouts  4.51 us

profile of v2, /device:TPU:97, one launch (start us, length us, event | category | flops | bytes accessed | tf_op | source)
XLA Modules:
  0.0 116.7 jit_solution(2723345498819104242)
XLA Ops:
  1.9 110.2 %step.1 = (bf16[384,2048]{1,0:T(8,128)(2,1)}, f32[128,1536]{1,0:T(8,128)}, f32[64,2048]{1,0:T(8,128)}) custom-call(bf16[2,384,2048]{2,1,0:T(8,128)(2,1)} %bitcast.9, bf16[2,384,2048]{2,1,0:T(8,128)(2,1)} %bitcast.10, bf16[2,384,1024]{2,1,0:T(8,128)(2,1)} %bitcast.12, bf16[2,384,1536]{2,1,0:T(8,128)(2,1)} %bitcast.11, bf16[128,1536]{1,0:T(8,128)(2,1)} %bitcast.16, ...), custom_call_target="tpu_custom_call" | custom-call | tf_op jit(solution)/shard_map/step/pallas_call | solution.py:500
  112.2 0.0 copy-start
  112.2 0.0 copy-start.1
  112.2 2.8 %copy.19 = bf16[1,384,2048]{2,1,0:T(8,128)(2,1)} copy(bf16[1,384,2048]{2,1,0:T(8,128)(2,1)} %bitcast.13) | data formatting | bytes 3145728
  115.0 0.0 copy-done
  115.0 0.9 copy.20
  115.9 0.0 copy-done.1
  115.9 0.8 copy.21
Async XLA Ops:
  112.2 2.9 %copy-start = (f32[128,1536]{1,0:T(8,128)S(1)}, f32[128,1536]{1,0:T(8,128)}, u32[]{:S(2)}) copy-start(f32[128,1536]{1,0:T(8,128)} %get-tuple-element.7) | copy-start | bytes 2359300
  112.2 3.7 %copy-start.1 = (f32[64,2048]{1,0:T(8,128)S(1)}, f32[64,2048]{1,0:T(8,128)}, u32[]{:S(2)}) copy-start(f32[64,2048]{1,0:T(8,128)} %get-tuple-element.8) | copy-start | bytes 1572868

commit v3 on v2

v3 whole, which is shorter than its diff:
```python
import functools

import jax
import jax.numpy as jnp
import numpy as np
from jax import lax
from jax.experimental import pallas as pl
from jax.experimental.pallas import tpu as pltpu
from jax.sharding import PartitionSpec as P

D = 2048
HEAD_DIM = 64
HEADS = 16
KV_HEADS = 4
SEQ = 384
QW = 1024
QKVW = 1536
CHIPS = 8
EPS = 1e-05
SCALE = HEAD_DIM ** (-0.5)
BF = jnp.bfloat16
F32 = jnp.float32
MESH = pl.DeviceIdType.MESH

Q_X, Q_YP, Q_YM, Q_PP, Q_PM, Q_RO, Q_RP = range(7)
O_YP, O_YM, O_X0, O_XP, O_XM, O_X2, O_RA, O_RB = range(7, 15)
SIB_Q = 15
SIB_O = 23
RS_SIB_Q, RS_SIB_O = 31, 32
R1_Q, R1_O = 33, 35
R2_Q, R2_O = 37, 41
RX_Q, RX_O = 45, 46
PERM = 47
Q_PP2, Q_PM2, Q_RP2 = 51, 52, 53
XB_S = 54
R1_B = 55
R2_B = 57
N_SEM = 61
XROWS = 16
LOW = 64 - XROWS


def rope_tables():
    half = HEAD_DIM // 2
    freq = 500000.0 ** (-2.0 * np.arange(half) / HEAD_DIM)
    ang = np.arange(SEQ)[:, None] * freq[None, :]
    cos = np.tile(np.cos(ang), (1, 4)).astype(np.float32)
    sin = np.tile(np.sin(ang), (1, 4)).astype(np.float32)
    sign = np.where(np.arange(128) % 64 < 32, -1.0, 1.0).astype(np.float32)
    return cos, sin * sign[None, :]


def dot(a, b, ca, cb):
    return lax.dot_general(a, b, (((ca,), (cb,)), ((), ())), preferred_element_type=F32)


def kernel(
    x_hbm, g_hbm, a_hbm, p_hbm, wq_hbm, wo_hbm, gain_hbm, b_hbm, w_hbm, cos_hbm, sin_hbm,
    prev_ref, gq_ref, go_ref,
    X, G, A, PG, WQ, WO, DQ, DO, SQ, SO, R1Q, R1O, R2Q, R2O, RXQ, RXO, XB, R1B, R2B,
    N, INV, QKV, QS, GS, KD, VD, GP, DK, DV, U, DOT, OUT,
    gain_ref, cos_ref, sin_ref, b_ref, w_ref,
    lsem, ssem, rsem, ready,
):
    s = lax.axis_index("section")
    f = lax.axis_index("fsdp")
    xh, y, c = f // 8, (f // 2) % 4, f % 2
    up, down, far = (y + 1) % 4, (y + 3) % 4, (y + 2) % 4
    oc, ox = 1 - c, 1 - xh
    n_sec = lax.axis_size("section")

    def dev(xx, yy, cc):
        return (s, xx * 8 + yy * 2 + cc)

    d_up, d_down, d_x, d_sib = dev(xh, up, c), dev(xh, down, c), dev(ox, y, c), dev(xh, y, oc)
    d_prev, d_next = (lax.rem(s + n_sec - 1, n_sec), f), (lax.rem(s + 1, n_sec), f)

    def qs(ref, xx, yy, cc, lo=0, n=128):
        return ref.at[xx * 4 + yy, pl.ds(pl.multiple_of(cc * 128 + lo, 64), n), :]

    def os(ref, xx, yy, cc, lo=0, n=64):
        return ref.at[xx * 4 + yy, pl.ds(pl.multiple_of(cc * 64 + lo, 16), n), :]

    started = []
    scope = []

    def phase(name):
        if scope:
            scope.pop().__exit__(None, None, None)
        if name:
            scope.append(jax.named_scope(name))
            scope[-1].__enter__()

    def rcopy(src, dst, slot, device):
        return pltpu.make_async_remote_copy(
            src_ref=src, dst_ref=dst, send_sem=ssem.at[slot], recv_sem=rsem.at[slot],
            device_id=device, device_id_type=MESH,
        )

    def send(src, dst, slot, device):
        cp = rcopy(src, dst, slot, device)
        cp.start()
        started.append(cp)

    def recv(dst, slot):
        rcopy(dst, dst, slot, d_sib).wait_recv()

    def gather(ref, shard, slot, device, src=None):
        send(shard if src is None else src, shard, slot, device)

    phase("entry")
    barrier = pltpu.get_barrier_semaphore()
    for d in (d_up, d_down, d_x, d_sib, d_prev):
        pl.semaphore_signal(barrier, inc=1, device_id=d, device_id_type=MESH)
    loads = [
        pltpu.make_async_copy(g_hbm, G, lsem.at[0]),
        pltpu.make_async_copy(a_hbm, A, lsem.at[1]),
        pltpu.make_async_copy(x_hbm, X, lsem.at[2]),
        pltpu.make_async_copy(p_hbm, PG, lsem.at[3]),
        pltpu.make_async_copy(wq_hbm, qs(WQ, xh, y, c), lsem.at[4]),
        pltpu.make_async_copy(wo_hbm, os(WO, xh, y, c), lsem.at[5]),
        pltpu.make_async_copy(gain_hbm, gain_ref, lsem.at[6]),
        pltpu.make_async_copy(cos_hbm, cos_ref, lsem.at[7]),
        pltpu.make_async_copy(sin_hbm, sin_ref, lsem.at[8]),
        pltpu.make_async_copy(b_hbm, b_ref, lsem.at[9]),
        pltpu.make_async_copy(w_hbm, w_ref, lsem.at[10]),
    ]
    for i in (9, 10, 4, 5, 0, 1, 6, 2, 3, 7, 8):
        cp = loads[i]
        cp.start()
    pl.semaphore_wait(barrier, 5)
    pl.semaphore_signal(ready, inc=1, device_id=d_next, device_id_type=MESH)

    phase("own_out")
    mine_q, mine_o = qs(WQ, xh, y, c), os(WO, xh, y, c)
    gather(WQ, mine_q, Q_X, d_x, wq_hbm)
    gather(WQ, mine_q, Q_YP, d_up, wq_hbm)
    gather(WQ, mine_q, Q_YM, d_down, wq_hbm)
    gather(WO, mine_o, O_YP, d_up, wo_hbm)
    gather(WO, mine_o, O_YM, d_down, wo_hbm)
    gather(WO, mine_o, O_X0, d_x, wo_hbm)
    gather(WQ, mine_q, SIB_Q + 0, d_sib, wq_hbm)
    gather(WO, mine_o, SIB_O + 0, d_sib, wo_hbm)

    loads[9].wait()
    loads[10].wait()
    b_slot, w_slot = b_ref[0], w_ref[0]

    phase("dw_out")
    loads[0].wait()
    loads[1].wait()

    def out_part(j, carry):
        lhs = A[w_slot, :, pl.ds(pl.multiple_of(j * 256, 256), 256)]
        part = dot(lhs, G[w_slot], 0, 0).astype(BF)
        DO[pl.ds(2 * j, 2)] = part.reshape(2, 128, D)
        return carry

    lax.fori_loop(0, 4, out_part, 0)
    send(DO.at[:, pl.ds(pl.multiple_of(oc * 64, 64), 64), :], SO, RS_SIB_O, d_sib)
    phase("norm_w")
    loads[2].wait()
    loads[3].wait()
    loads[6].wait()

    def norm(slot):
        def rows(r, carry):
            sl = pl.ds(pl.multiple_of(r * 16, 16), 16)
            wide = X[slot, sl, :].astype(F32)
            inv = lax.rsqrt(jnp.mean(wide * wide, axis=-1, keepdims=True) + EPS)
            INV[sl, :] = jnp.broadcast_to(inv, (16, 128))
            N[sl, :] = (wide * inv * gain_ref[...]).astype(BF)
            return carry

        lax.fori_loop(0, SEQ // 16, rows, 0, unroll=4)

    norm(w_slot)

    phase("dw_qkv")

    def qkv_part(j, carry):
        lhs = N[:, pl.ds(pl.multiple_of(j * 256, 256), 256)]
        DQ[j] = dot(lhs, PG[w_slot], 0, 0).astype(BF)
        return carry

    lax.fori_loop(0, CHIPS, qkv_part, 0)
    send(DQ.at[:, pl.ds(pl.multiple_of(oc * 128, 128), 128), :], SQ, RS_SIB_Q, d_sib)
    phase("norm_b")
    norm(b_slot)

    lane = lax.broadcasted_iota(jnp.int32, (128, 128), 1)
    first_half = lane % 64 < 32
    low = lane < 64

    def acc_qkv(xx, yy, first=False):
        j = xx * 4 + yy
        part = dot(N[:, pl.ds(pl.multiple_of(j * 256, 256), 256)], WQ[j], 1, 0)
        QKV[...] = part if first else QKV[...] + part

    def stack(ref, b, kv, i, tile):
        zero = jnp.zeros_like(tile)
        ref[kv, b, pl.ds(pl.multiple_of(i * 128, 128), 64)] = jnp.where(low[:64], tile, zero)
        ref[kv, b, pl.ds(pl.multiple_of(i * 128 + 64, 64), 64)] = jnp.where(low[:64], zero, tile)

    def attn_grad(xx, yy):
        j = xx * 4 + yy
        tile = dot(G[b_slot], WO[j], 1, 1).astype(BF)
        for b in range(6):
            stack(GS, b, j // 2, j % 2, tile[b * 64 : (b + 1) * 64])

    def pair_sum_o(j, carry):
        so = pl.ds(pl.multiple_of(c * 64, 64), 64)
        DO[j, so, :] = (DO[j, so, :].astype(F32) + SO[j].astype(F32)).astype(BF)
        return carry

    def pair_sum_q(j, carry):
        sq = pl.ds(pl.multiple_of(c * 128, 128), 128)
        DQ[j, sq, :] = (DQ[j, sq, :].astype(F32) + SQ[j].astype(F32)).astype(BF)
        return carry

    sgn = 1 - 2 * xh
    ya, yb = (y + 4 - sgn) % 4, (y + 4 + sgn) % 4
    phase("fwd_xq")
    part_q = qs(WQ, ox, y, c)
    recv(part_q, Q_X)
    gather(WQ, qs(WQ, ox, y, c, 0, 64), Q_PP, d_up)
    gather(WQ, qs(WQ, ox, y, c, 0, 64), Q_PM, d_down)
    gather(WQ, part_q, SIB_Q + 1, d_sib)
    phase("fwd_yq")
    from_down, from_up = qs(WQ, xh, down, c), qs(WQ, xh, up, c)
    recv(from_down, Q_YP)
    recv(from_up, Q_YM)
    gather(WQ, from_down, SIB_Q + 2, d_sib)
    gather(WQ, from_up, SIB_Q + 3, d_sib)
    phase("sum_o")
    recv(SO, RS_SIB_O)
    lax.fori_loop(0, CHIPS, pair_sum_o, 0)
    phase("qkv_0")
    loads[4].wait()
    recv(mine_q, SIB_Q + 0)
    acc_qkv(xh, y, first=True)
    recv(mine_q, SIB_Q + 1)
    acc_qkv(ox, y)
    phase("fwd_yo")
    o_down, o_up = os(WO, xh, down, c), os(WO, xh, up, c)
    recv(o_down, O_YP)
    recv(o_up, O_YM)
    gather(WO, os(WO, xh, down, c, 0, 32), O_RA, d_up)
    gather(WO, os(WO, xh, up, c, 32, 32), O_RB, d_down)
    gather(WQ, qs(WQ, ox, y, c, 64, 64), Q_PP2, d_up)
    gather(WQ, qs(WQ, ox, y, c, 64, 64), Q_PM2, d_down)
    gather(WO, o_down, O_XP, d_x)
    gather(WO, o_up, O_XM, d_x)
    gather(WQ, qs(WQ, xh, ya, c), Q_RO, dev(xh, yb, c))
    gather(WO, o_down, SIB_O + 1, d_sib)
    gather(WO, o_up, SIB_O + 2, d_sib)
    o_part = os(WO, ox, y, c)
    recv(o_part, O_X0)
    gather(WO, o_part, SIB_O + 4, d_sib)
    phase("qkv_1")
    recv(mine_q, SIB_Q + 2)
    acc_qkv(xh, down)
    recv(mine_q, SIB_Q + 3)
    acc_qkv(xh, up)
    phase("ag_0")
    loads[5].wait()
    recv(mine_o, SIB_O + 0)
    attn_grad(xh, y)
    recv(mine_o, SIB_O + 1)
    attn_grad(xh, down)
    recv(mine_o, SIB_O + 2)
    attn_grad(xh, up)
    recv(mine_o, SIB_O + 4)
    attn_grad(ox, y)

    phase("fwd_yp1")
    recv(qs(WQ, ox, down, c, 0, 64), Q_PP)
    recv(qs(WQ, ox, up, c, 0, 64), Q_PM)
    gather(WQ, qs(WQ, ox, yb, c, 0, 64), Q_RP, dev(xh, ya, c))
    phase("fwd_ofar")
    o_far = os(WO, xh, far, c)
    recv(os(WO, xh, far, c, 0, 32), O_RA)
    recv(os(WO, xh, far, c, 32, 32), O_RB)
    gather(WO, o_far, O_X2, d_x)
    gather(WO, o_far, SIB_O + 3, d_sib)
    phase("fwd_yp")
    part_down, part_up = qs(WQ, ox, down, c), qs(WQ, ox, up, c)
    recv(qs(WQ, ox, down, c, 64, 64), Q_PP2)
    recv(qs(WQ, ox, up, c, 64, 64), Q_PM2)
    gather(WQ, qs(WQ, ox, yb, c, 64, 64), Q_RP2, dev(xh, ya, c))
    gather(WQ, part_down, SIB_Q + 4, d_sib)
    gather(WQ, part_up, SIB_Q + 5, d_sib)

    def pass_o(yy, slot, i):
        piece = os(WO, ox, yy, c)
        recv(piece, slot)
        gather(WO, piece, SIB_O + i, d_sib)

    pass_o(down, O_XP, 5)
    phase("sum_q")
    recv(SQ, RS_SIB_Q)
    lax.fori_loop(0, CHIPS, pair_sum_q, 0)
    send(qs(DQ, 0, far, c), R1Q.at[0], R1_Q + 0, d_up)
    send(qs(DQ, 1, far, c), R1Q.at[1], R1_Q + 1, d_down)
    send(os(DO, 0, far, c, 0, LOW), R1O.at[0], R1_O + 0, d_up)
    send(os(DO, 1, far, c, 0, LOW), R1O.at[1], R1_O + 1, d_down)
    send(qs(DQ, 1, up, c), R2Q.at[0, 1], R2_Q + 1, d_up)
    send(qs(DQ, 0, down, c), R2Q.at[1, 0], R2_Q + 2, d_down)
    phase("ag_1")
    recv(mine_o, SIB_O + 5)
    attn_grad(ox, down)
    phase("qkv_2")
    recv(mine_q, SIB_Q + 4)
    acc_qkv(ox, down)
    recv(mine_q, SIB_Q + 5)
    acc_qkv(ox, up)
    phase("fwd_xo")
    pass_o(up, O_XM, 6)
    phase("ag_2")
    recv(mine_o, SIB_O + 3)
    attn_grad(xh, far)
    recv(mine_o, SIB_O + 6)
    attn_grad(ox, up)
    phase("fwd_qfar")
    pass_o(far, O_X2, 7)
    send(
        DO.at[pl.ds(ox * 4, 4), pl.ds(pl.multiple_of(c * 64 + LOW, 16), XROWS), :], XB, XB_S, d_x
    )
    far_own, far_part = qs(WQ, xh, far, c), qs(WQ, ox, far, c)
    recv(far_own, Q_RO)
    gather(WQ, far_own, SIB_Q + 6, d_sib)
    recv(qs(WQ, ox, far, c, 0, 64), Q_RP)
    recv(qs(WQ, ox, far, c, 64, 64), Q_RP2)
    gather(WQ, far_part, SIB_Q + 7, d_sib)
    phase("ag_3")
    recv(mine_o, SIB_O + 7)
    attn_grad(ox, far)
    phase("qkv_3")
    recv(mine_q, SIB_Q + 6)
    acc_qkv(xh, far)
    recv(mine_q, SIB_Q + 7)
    acc_qkv(ox, far)

    phase("rope")
    loads[7].wait()
    loads[8].wait()

    def rot(u):
        mask = first_half[: u.shape[0]]
        return jnp.where(mask, pltpu.roll(u, 96, 1), pltpu.roll(u, 32, 1))

    def rope(u, rows):
        return u * cos_ref[rows, :] + rot(u) * sin_ref[rows, :]

    def unrope(u, rows):
        return u * cos_ref[rows, :] - rot(u) * sin_ref[rows, :]

    def rope_q(b):
        rows = pl.ds(b * 64, 64)
        for t in range(8):
            u = QKV[rows, t * 128 : (t + 1) * 128]
            stack(QS, b, t // 2, t % 2, rope(u, rows).astype(BF))

    for qb in range(3):
        rows = pl.ds(qb * 128, 128)
        for base, dst in ((QW, KD), (QW + 256, VD)):
            for i in range(2):
                u = QKV[rows, base + i * 128 : base + (i + 1) * 128]
                if dst is KD:
                    u = rope(u, rows)
                r = pltpu.roll(u, 64, 1)
                dst[2 * i, rows, :] = jnp.where(low, u, r).astype(BF)
                dst[2 * i + 1, rows, :] = jnp.where(low, r, u).astype(BF)
    rope_q(5)

    exp_scale = SCALE * 1.4426950408889634

    def attend(b0, nb):
        n = nb * 64
        keys = b0 * 64 + n
        rows = pl.ds(b0 * 64, n)
        col = lax.broadcasted_iota(jnp.int32, (n, 4 * n), 1)
        diag = lax.broadcasted_iota(jnp.int32, (n, 4 * n), 0) <= (col // 256) * 64 + col % 64
        low_n = low[:n]

        def one_kv(kv, carry):
            kd, vd = KD[kv, :keys], VD[kv, :keys]
            q4 = QS[kv, b0 : b0 + nb].reshape(4 * n, 128)
            g4 = GS[kv, b0 : b0 + nb].reshape(4 * n, 128)
            e = jnp.exp2(dot(kd, q4, 1, 1) * exp_scale)
            last = jnp.where(diag, e[keys - n :], 0.0)
            e = last if b0 == 0 else jnp.concatenate([e[: keys - n], last], axis=0)
            probs = e * (1.0 / jnp.sum(e, axis=0, keepdims=True))
            dv = dot(probs.astype(BF), g4, 1, 0)
            dp = dot(vd, g4, 1, 1)
            delta = jnp.sum(probs * dp, axis=0, keepdims=True)
            ds = (probs * (dp - delta)).astype(BF)
            dk = dot(ds, q4, 1, 0) * SCALE
            dq = dot(ds, kd, 0, 0) * SCALE
            if keys == SEQ:
                DK[kv], DV[kv] = dk, dv
            else:
                DK[kv, :keys] += dk
                DV[kv, :keys] += dv
            for i in range(2):
                head = [
                    jnp.concatenate(
                        [dq[256 * k + 64 * h : 256 * k + 64 * h + 64] for k in range(nb)], axis=0
                    )
                    for h in (2 * i, 2 * i + 1)
                ]
                sl = pl.ds(pl.multiple_of((2 * kv + i) * 128, 128), 128)
                GP[:n, sl] = unrope(jnp.where(low_n, head[0], head[1]), rows).astype(BF)
            return carry

        lax.fori_loop(0, KV_HEADS, one_kv, 0, unroll=4)
        for i in range(2):
            for base, ref in ((QW, DK), (QW + 256, DV)):
                halves = []
                for kv in (2 * i, 2 * i + 1):
                    t = ref[kv, rows]
                    halves.append(t + pltpu.roll(t, 64, 1))
                tile = jnp.where(low_n, halves[0], halves[1])
                if ref is DK:
                    tile = unrope(tile, rows)
                GP[:n, base + i * 128 : base + (i + 1) * 128] = tile.astype(BF)

    def input_grad(b0, nb, slot):
        n = nb * 64
        rows = pl.ds(b0 * 64, n)
        DOT[...] = jnp.zeros_like(DOT)

        def normed_cols(j, carry):
            sl = pl.ds(pl.multiple_of(j * 256, 256), 256)
            u = dot(GP[:n], WQ[j], 1, 1) * gain_ref[:, sl]
            U[:n, sl] = u
            ux = u * X[b_slot, rows, sl].astype(F32)
            DOT[:n] += ux[:, :128] + ux[:, 128:]
            return carry

        lax.fori_loop(0, CHIPS, normed_cols, 0, unroll=2)
        phase(f"fin_{b0}")
        inv = INV[rows, :]
        mean = jnp.sum(DOT[:n], axis=-1, keepdims=True) * (1.0 / D)
        DOT[:n] = inv * inv * inv * mean

        def finish(j, carry):
            sl = pl.ds(pl.multiple_of(j * 128, 128), 128)
            for r in range(n // 32):
                part = pl.ds(32 * r, 32)
                here = pl.ds(b0 * 64 + 32 * r, 32)
                res = (
                    G[b_slot, here, sl].astype(F32)
                    + INV[here, :] * U[part, sl]
                    - X[b_slot, here, sl].astype(F32) * DOT[part, :]
                )
                OUT[here, sl] = res.astype(BF)
            return carry

        lax.fori_loop(0, 16, finish, 0, unroll=4)
        if slot == 0:
            pl.semaphore_wait(ready, 1)
        send(OUT.at[rows], prev_ref.at[rows], PERM + slot, d_prev)

    def add_into(dst, other):
        dst[...] = (dst[...].astype(F32) + other.astype(F32)).astype(BF)

    phase("attn_5")
    attend(5, 1)
    phase("ig_5")
    input_grad(5, 1, 0)
    phase("attn_4")
    rope_q(4)
    attend(4, 1)
    phase("ig_4")
    input_grad(4, 1, 1)

    phase("rs_relay_q")
    recv(R1Q.at[0], R1_Q + 0)
    add_into(qs(DQ, 0, up, c), R1Q[0])
    recv(R1Q.at[1], R1_Q + 1)
    add_into(qs(DQ, 1, down, c), R1Q[1])
    send(qs(DQ, 0, up, c), R2Q.at[0, 0], R2_Q + 0, d_up)
    send(qs(DQ, 1, down, c), R2Q.at[1, 1], R2_Q + 3, d_down)
    send(os(DO, 1, up, c, 0, LOW), R2O.at[0, 1], R2_O + 1, d_up)
    send(os(DO, 0, down, c, 0, LOW), R2O.at[1, 0], R2_O + 2, d_down)
    recv(XB, XB_S)
    for i in range(4):
        XB[i] = (XB[i].astype(F32) + os(DO, xh, i, c, LOW, XROWS)[...].astype(F32)).astype(BF)
    c0, c1 = pl.ds(0, D // 2), pl.ds(D // 2, D // 2)
    send(XB.at[far, :, c0], R1B.at[0], R1_B + 0, d_up)
    send(XB.at[far, :, c1], R1B.at[1], R1_B + 1, d_down)
    send(XB.at[up, :, c1], R2B.at[0, :, c1], R2_B + 1, d_up)
    send(XB.at[down, :, c0], R2B.at[1, :, c0], R2_B + 2, d_down)
    phase("attn_2")
    for b in range(4):
        rope_q(b)
    attend(2, 2)
    phase("ig_2")
    input_grad(2, 2, 2)
    phase("rs_relay_o")
    recv(R1O.at[0], R1_O + 0)
    add_into(os(DO, 0, up, c, 0, LOW), R1O[0])
    recv(R1O.at[1], R1_O + 1)
    add_into(os(DO, 1, down, c, 0, LOW), R1O[1])
    send(os(DO, 0, up, c, 0, LOW), R2O.at[0, 0], R2_O + 0, d_up)
    send(os(DO, 1, down, c, 0, LOW), R2O.at[1, 1], R2_O + 3, d_down)
    phase("attn_0")
    attend(0, 2)
    phase("ig_0")
    input_grad(0, 2, 3)

    phase("rs_wait_q")
    for i in range(4):
        recv(R2Q.at[i // 2, i % 2], R2_Q + i)
    phase("rs_tot_q")

    def total(mine, R2, xx):
        return mine[...].astype(F32) + R2[0, xx].astype(F32) + R2[1, xx].astype(F32)

    theirs = qs(DQ, ox, y, c)
    theirs[...] = total(theirs, R2Q, ox).astype(BF)
    gq_ref[...] = total(qs(DQ, xh, y, c), R2Q, xh)
    send(theirs, RXQ, RX_Q, d_x)
    phase("rs_relay_b")
    recv(R1B.at[0], R1_B + 0)
    add_into(XB.at[up, :, c0], R1B[0])
    recv(R1B.at[1], R1_B + 1)
    add_into(XB.at[down, :, c1], R1B[1])
    send(XB.at[up, :, c0], R2B.at[0, :, c0], R2_B + 0, d_up)
    send(XB.at[down, :, c1], R2B.at[1, :, c1], R2_B + 3, d_down)
    phase("rs_wait_o")
    for i in range(4):
        recv(R2O.at[i // 2, i % 2], R2_O + i)
    theirs = os(DO, ox, y, c, 0, LOW)
    theirs[...] = total(theirs, R2O, ox).astype(BF)
    go_ref[:LOW] = total(os(DO, xh, y, c, 0, LOW), R2O, xh)
    send(theirs, RXO, RX_O, d_x)
    for i in range(4):
        recv(R1B.at[0], R2_B + i)
    go_ref[LOW:] = XB[y].astype(F32) + R2B[0].astype(F32) + R2B[1].astype(F32)
    phase("rs_x_wait")
    recv(RXQ, RX_Q)
    gq_ref[...] += RXQ[...].astype(F32)
    recv(RXO, RX_O)
    go_ref[:LOW] += RXO[...].astype(F32)
    phase("perm_wait")
    for k, (b, nb) in enumerate(((5, 1), (4, 1), (2, 2), (0, 2))):
        recv(prev_ref.at[pl.ds(64 * b, 64 * nb)], PERM + k)
    phase("send_wait")
    for cp in started:
        cp.wait_send()
    phase(None)


def local(x, g, a, p, wq, wo, gain, b, w):
    cos, sin = rope_tables()
    any_ = pl.BlockSpec(memory_space=pl.ANY)
    vm = pl.BlockSpec(memory_space=pltpu.VMEM)
    hbm = pl.BlockSpec(memory_space=pltpu.HBM)
    V = pltpu.VMEM
    prev, gq, go = pl.pallas_call(
        kernel,
        name="step",
        out_shape=(
            pltpu.VMEM((SEQ, D), BF),
            pltpu.VMEM((128, QKVW), F32),
            pltpu.VMEM((64, D), F32),
        ),
        in_specs=[any_] * 7 + [hbm] * 2 + [any_] * 2,
        out_specs=(vm, vm, vm),
        scratch_shapes=[
            V((2, SEQ, D), BF), V((2, SEQ, D), BF), V((2, SEQ, QW), BF), V((2, SEQ, QKVW), BF),
            V((CHIPS, 256, QKVW), BF), V((CHIPS, 128, D), BF),
            V((CHIPS, 256, QKVW), BF), V((CHIPS, 128, D), BF),
            V((CHIPS, 128, QKVW), BF), V((CHIPS, 64, D), BF),
            V((2, 128, QKVW), BF), V((2, LOW, D), BF),
            V((2, 2, 128, QKVW), BF), V((2, 2, LOW, D), BF),
            V((128, QKVW), BF), V((LOW, D), BF),
            V((4, XROWS, D), BF), V((2, XROWS, D // 2), BF), V((2, XROWS, D), BF),
            V((SEQ, D), BF), V((SEQ, 128), F32), V((SEQ, QKVW), F32),
            V((KV_HEADS, 6, 256, 128), BF), V((KV_HEADS, 6, 256, 128), BF),
            V((KV_HEADS, SEQ, 128), BF), V((KV_HEADS, SEQ, 128), BF),
            V((128, QKVW), BF), V((KV_HEADS, SEQ, 128), F32), V((KV_HEADS, SEQ, 128), F32),
            V((128, D), F32), V((128, 128), F32), V((SEQ, D), BF),
            V((1, D), F32), V((SEQ, 128), F32), V((SEQ, 128), F32),
            pltpu.SMEM((1,), jnp.int32), pltpu.SMEM((1,), jnp.int32),
            pltpu.SemaphoreType.DMA((11,)),
            pltpu.SemaphoreType.DMA((N_SEM,)),
            pltpu.SemaphoreType.DMA((N_SEM,)),
            pltpu.SemaphoreType.REGULAR,
        ],
        compiler_params=pltpu.CompilerParams(
            collective_id=0, has_side_effects=True, vmem_limit_bytes=59 * 1024 * 1024
        ),
    )(
        x[0], g[0], a[0], p[0], wq[0], wo[0], gain, b, w, jnp.asarray(cos), jnp.asarray(sin)
    )
    return prev[None], gq[None], go[None]


def solution(mesh):
    row = P("section", None, "fsdp", None)
    out = P("section", "fsdp", None)
    return jax.shard_map(
        local,
        mesh=mesh,
        in_specs=(row, row, row, row, out, out, P("section", None), P("section"), P("section")),
        out_specs=(out, out, out),
        check_vma=False,
    )
```

time: 117 us -> 107 us (0.915)
  Pallas kernels: 110 us -> 102 us
  local copies, waits for them, and re-layouts: 4.51 us -> 2.82 us
    pallas_call x1, Pallas kernels: 110 us -> 102 us  [local(): pl.pallas_call(kernel, name='step', out_shape=(pltpu.VMEM((SEQ, D), BF),...]
    unnamed x7 -> x3, local copies, waits for them, and re-layouts: 4.51 us -> 2.82 us
where the time goes in v3:
time: 107 us
  Pallas kernels  102 us (95%)
  local copies, waits for them, and re-layouts  2.82 us (3%)
  between operations  1.93 us (2%)
    pallas_call x1, Pallas kernels, local(): pl.pallas_call(kernel, name='step', out_shape=(pltpu.VMEM((SEQ, D), BF),...  102 us
    unnamed x3, local copies, waits for them, and re-layouts  2.82 us

profile of v3, /device:TPU:97, one launch (start us, length us, event | category | flops | bytes accessed | tf_op | source)
XLA Modules:
  0.0 107.0 jit_solution(7013945637069644394)
XLA Ops:
  1.9 102.2 %step.1 = (bf16[384,2048]{1,0:T(8,128)(2,1)S(1)}, f32[128,1536]{1,0:T(8,128)S(1)}, f32[64,2048]{1,0:T(8,128)S(1)}) custom-call(bf16[2,384,2048]{2,1,0:T(8,128)(2,1)} %bitcast.12, bf16[2,384,2048]{2,1,0:T(8,128)(2,1)} %bitcast.13, bf16[2,384,1024]{2,1,0:T(8,128)(2,1)} %bitcast.15, bf16[2,384,1536]{2,1,0:T(8,128)(2,1)} %bitcast.14, ...), custom_call_target="tpu_custom_call" | custom-call | tf_op jit(solution)/shard_map/step/pallas_call | solution.py:562
  104.2 1.1 %copy.17 = bf16[1,384,2048]{2,1,0:T(8,128)(2,1)} copy(bf16[1,384,2048]{2,1,0:T(8,128)(2,1)S(1)} %bitcast.9) | data formatting | bytes 3145728
  105.3 0.9 copy.18
  106.2 0.8 copy.19

commit v4 on v3

--- a/solution.py
+++ b/solution.py
@@ -30,12 +30,13 @@
 R1_Q, R1_O = 33, 35
 R2_Q, R2_O = 37, 41
 RX_Q, RX_O = 45, 46
-PERM = 47
+PERM = 61
 Q_PP2, Q_PM2, Q_RP2 = 51, 52, 53
 XB_S = 54
 R1_B = 55
 R2_B = 57
-N_SEM = 61
+Q_RO2, SIB_Q6B, SIB_Q7B = 66, 67, 68
+N_SEM = 69
 XROWS = 16
 LOW = 64 - XROWS
 
@@ -55,11 +56,11 @@
 
 
 def kernel(
-    x_hbm, g_hbm, a_hbm, p_hbm, wq_hbm, wo_hbm, gain_hbm, b_hbm, w_hbm, cos_hbm, sin_hbm,
+    x_hbm, g_hbm, a_hbm, p_hbm, wq_hbm, wo_hbm, gain_hbm, sched_ref, cos_hbm, sin_hbm,
     prev_ref, gq_ref, go_ref,
-    X, G, A, PG, WQ, WO, DQ, DO, SQ, SO, R1Q, R1O, R2Q, R2O, RXQ, RXO, XB, R1B, R2B,
+    X, G, A, PG, WQ, WO, DQ, DO, SQ, SO, R1Q, R1O, R2Q, R2O, RXQ, RXO, XB, R1B, R2B, WT,
     N, INV, QKV, QS, GS, KD, VD, GP, DK, DV, U, DOT, OUT,
-    gain_ref, cos_ref, sin_ref, b_ref, w_ref,
+    gain_ref, cos_ref, sin_ref,
     lsem, ssem, rsem, ready,
 ):
     s = lax.axis_index("section")
@@ -105,8 +106,8 @@
     def recv(dst, slot):
         rcopy(dst, dst, slot, d_sib).wait_recv()
 
-    def gather(ref, shard, slot, device, src=None):
-        send(shard if src is None else src, shard, slot, device)
+    def gather(ref, shard, slot, device):
+        send(shard, shard, slot, device)
 
     phase("entry")
     barrier = pltpu.get_barrier_semaphore()
@@ -122,10 +123,8 @@
         pltpu.make_async_copy(gain_hbm, gain_ref, lsem.at[6]),
         pltpu.make_async_copy(cos_hbm, cos_ref, lsem.at[7]),
         pltpu.make_async_copy(sin_hbm, sin_ref, lsem.at[8]),
-        pltpu.make_async_copy(b_hbm, b_ref, lsem.at[9]),
-        pltpu.make_async_copy(w_hbm, w_ref, lsem.at[10]),
     ]
-    for i in (9, 10, 4, 5, 0, 1, 6, 2, 3, 7, 8):
+    for i in (4, 5, 0, 1, 6, 2, 3, 7, 8):
         cp = loads[i]
         cp.start()
     pl.semaphore_wait(barrier, 5)
@@ -133,18 +132,19 @@
 
     phase("own_out")
     mine_q, mine_o = qs(WQ, xh, y, c), os(WO, xh, y, c)
-    gather(WQ, mine_q, Q_X, d_x, wq_hbm)
-    gather(WQ, mine_q, Q_YP, d_up, wq_hbm)
-    gather(WQ, mine_q, Q_YM, d_down, wq_hbm)
-    gather(WO, mine_o, O_YP, d_up, wo_hbm)
-    gather(WO, mine_o, O_YM, d_down, wo_hbm)
-    gather(WO, mine_o, O_X0, d_x, wo_hbm)
-    gather(WQ, mine_q, SIB_Q + 0, d_sib, wq_hbm)
-    gather(WO, mine_o, SIB_O + 0, d_sib, wo_hbm)
-
-    loads[9].wait()
-    loads[10].wait()
-    b_slot, w_slot = b_ref[0], w_ref[0]
+    loads[4].wait()
+    gather(WQ, mine_q, Q_YP, d_up)
+    gather(WQ, mine_q, Q_YM, d_down)
+    gather(WQ, mine_q, Q_X, d_x)
+    loads[5].wait()
+    gather(WO, mine_o, O_YP, d_up)
+    gather(WO, mine_o, O_YM, d_down)
+    gather(WO, mine_o, O_X0, d_x)
+    gather(WQ, mine_q, SIB_Q + 0, d_sib)
+    gather(WO, mine_o, SIB_O + 0, d_sib)
+
+    sched = sched_ref[0]
+    b_slot, w_slot = sched % 2, sched // 2
 
     phase("dw_out")
     loads[0].wait()
@@ -196,6 +196,9 @@
         j = xx * 4 + yy
         part = dot(N[:, pl.ds(pl.multiple_of(j * 256, 256), 256)], WQ[j], 1, 0)
         QKV[...] = part if first else QKV[...] + part
+
+    def flip(xx, yy, k):
+        WT[k] = jnp.transpose(WQ[xx * 4 + yy])
 
     def stack(ref, b, kv, i, tile):
         zero = jnp.zeros_like(tile)
@@ -236,11 +239,12 @@
     recv(SO, RS_SIB_O)
     lax.fori_loop(0, CHIPS, pair_sum_o, 0)
     phase("qkv_0")
-    loads[4].wait()
     recv(mine_q, SIB_Q + 0)
     acc_qkv(xh, y, first=True)
     recv(mine_q, SIB_Q + 1)
     acc_qkv(ox, y)
+    flip(xh, y, 0)
+    flip(ox, y, 1)
     phase("fwd_yo")
     o_down, o_up = os(WO, xh, down, c), os(WO, xh, up, c)
     recv(o_down, O_YP)
@@ -251,7 +255,8 @@
     gather(WQ, qs(WQ, ox, y, c, 64, 64), Q_PM2, d_down)
     gather(WO, o_down, O_XP, d_x)
     gather(WO, o_up, O_XM, d_x)
-    gather(WQ, qs(WQ, xh, ya, c), Q_RO, dev(xh, yb, c))
+    gather(WQ, qs(WQ, xh, ya, c, 0, 64), Q_RO, dev(xh, yb, c))
+    gather(WQ, qs(WQ, xh, ya, c, 64, 64), Q_RO2, dev(xh, yb, c))
     gather(WO, o_down, SIB_O + 1, d_sib)
     gather(WO, o_up, SIB_O + 2, d_sib)
     o_part = os(WO, ox, y, c)
@@ -263,7 +268,6 @@
     recv(mine_q, SIB_Q + 3)
     acc_qkv(xh, up)
     phase("ag_0")
-    loads[5].wait()
     recv(mine_o, SIB_O + 0)
     attn_grad(xh, y)
     recv(mine_o, SIB_O + 1)
@@ -272,6 +276,7 @@
     attn_grad(xh, up)
     recv(mine_o, SIB_O + 4)
     attn_grad(ox, y)
+    flip(xh, down, 4)
 
     phase("fwd_yp1")
     recv(qs(WQ, ox, down, c, 0, 64), Q_PP)
@@ -283,6 +288,8 @@
     recv(os(WO, xh, far, c, 32, 32), O_RB)
     gather(WO, o_far, O_X2, d_x)
     gather(WO, o_far, SIB_O + 3, d_sib)
+    phase("flip_3")
+    flip(xh, up, 2)
     phase("fwd_yp")
     part_down, part_up = qs(WQ, ox, down, c), qs(WQ, ox, up, c)
     recv(qs(WQ, ox, down, c, 64, 64), Q_PP2)
@@ -316,29 +323,39 @@
     acc_qkv(ox, up)
     phase("fwd_xo")
     pass_o(up, O_XM, 6)
-    phase("ag_2")
-    recv(mine_o, SIB_O + 3)
-    attn_grad(xh, far)
-    recv(mine_o, SIB_O + 6)
-    attn_grad(ox, up)
-    phase("fwd_qfar")
-    pass_o(far, O_X2, 7)
     send(
         DO.at[pl.ds(ox * 4, 4), pl.ds(pl.multiple_of(c * 64 + LOW, 16), XROWS), :], XB, XB_S, d_x
     )
-    far_own, far_part = qs(WQ, xh, far, c), qs(WQ, ox, far, c)
-    recv(far_own, Q_RO)
-    gather(WQ, far_own, SIB_Q + 6, d_sib)
-    recv(qs(WQ, ox, far, c, 0, 64), Q_RP)
-    recv(qs(WQ, ox, far, c, 64, 64), Q_RP2)
-    gather(WQ, far_part, SIB_Q + 7, d_sib)
+    phase("ag_2")
+
+    def pass_far(xx, lo, slot, sib):
+        piece = qs(WQ, xx, far, c, lo, 64)
+        recv(piece, slot)
+        gather(WQ, piece, sib, d_sib)
+
+    recv(mine_o, SIB_O + 3)
+    attn_grad(xh, far)
+    pass_far(xh, 0, Q_RO, SIB_Q + 6)
+    pass_far(ox, 0, Q_RP, SIB_Q + 7)
+    recv(mine_o, SIB_O + 6)
+    attn_grad(ox, up)
+    pass_o(far, O_X2, 7)
+    phase("flip_45")
+    flip(ox, down, 5)
+    flip(ox, up, 3)
+    phase("fwd_qfar")
+    pass_far(xh, 64, Q_RO2, SIB_Q6B)
+    pass_far(ox, 64, Q_RP2, SIB_Q7B)
     phase("ag_3")
     recv(mine_o, SIB_O + 7)
     attn_grad(ox, far)
     phase("qkv_3")
-    recv(mine_q, SIB_Q + 6)
+    half_q = qs(WQ, xh, y, c, 0, 64)
+    recv(half_q, SIB_Q + 6)
+    recv(half_q, SIB_Q6B)
     acc_qkv(xh, far)
-    recv(mine_q, SIB_Q + 7)
+    recv(half_q, SIB_Q + 7)
+    recv(half_q, SIB_Q7B)
     acc_qkv(ox, far)
 
     phase("rope")
@@ -396,7 +413,7 @@
             delta = jnp.sum(probs * dp, axis=0, keepdims=True)
             ds = (probs * (dp - delta)).astype(BF)
             dk = dot(ds, q4, 1, 0) * SCALE
-            dq = dot(ds, kd, 0, 0) * SCALE
+            dq = jnp.transpose(dot(kd, ds, 0, 0)) * SCALE
             if keys == SEQ:
                 DK[kv], DV[kv] = dk, dv
             else:
@@ -430,15 +447,24 @@
         rows = pl.ds(b0 * 64, n)
         DOT[...] = jnp.zeros_like(DOT)
 
-        def normed_cols(j, carry):
+        def use(j, u):
             sl = pl.ds(pl.multiple_of(j * 256, 256), 256)
-            u = dot(GP[:n], WQ[j], 1, 1) * gain_ref[:, sl]
+            u = u * gain_ref[:, sl]
             U[:n, sl] = u
             ux = u * X[b_slot, rows, sl].astype(F32)
             DOT[:n] += ux[:, :128] + ux[:, 128:]
+
+        def normed_cols(k, carry):
+            t = k // 2
+            use((xh + k) % 2 * 4 + (y + t + t // 2) % 4, dot(GP[:n], WT[k], 1, 0))
             return carry
 
-        lax.fori_loop(0, CHIPS, normed_cols, 0, unroll=2)
+        def far_cols(xx, carry):
+            use(xx * 4 + far, dot(GP[:n], WQ[xx * 4 + far], 1, 1))
+            return carry
+
+        lax.fori_loop(0, 6, normed_cols, 0, unroll=2)
+        lax.fori_loop(0, 2, far_cols, 0, unroll=2)
         phase(f"fin_{b0}")
         inv = INV[rows, :]
         mean = jnp.sum(DOT[:n], axis=-1, keepdims=True) * (1.0 / D)
@@ -492,12 +518,16 @@
     send(XB.at[far, :, c1], R1B.at[1], R1_B + 1, d_down)
     send(XB.at[up, :, c1], R2B.at[0, :, c1], R2_B + 1, d_up)
     send(XB.at[down, :, c0], R2B.at[1, :, c0], R2_B + 2, d_down)
-    phase("attn_2")
+    phase("attn_3")
     for b in range(4):
         rope_q(b)
-    attend(2, 2)
+    attend(3, 1)
+    phase("ig_3")
+    input_grad(3, 1, 2)
+    phase("attn_2")
+    attend(2, 1)
     phase("ig_2")
-    input_grad(2, 2, 2)
+    input_grad(2, 1, 3)
     phase("rs_relay_o")
     recv(R1O.at[0], R1_O + 0)
     add_into(os(DO, 0, up, c, 0, LOW), R1O[0])
@@ -508,7 +538,7 @@
     phase("attn_0")
     attend(0, 2)
     phase("ig_0")
-    input_grad(0, 2, 3)
+    input_grad(0, 2, 4)
 
     phase("rs_wait_q")
     for i in range(4):
@@ -545,7 +575,7 @@
     recv(RXO, RX_O)
     go_ref[:LOW] += RXO[...].astype(F32)
     phase("perm_wait")
-    for k, (b, nb) in enumerate(((5, 1), (4, 1), (2, 2), (0, 2))):
+    for k, (b, nb) in enumerate(((5, 1), (4, 1), (3, 1), (2, 1), (0, 2))):
         recv(prev_ref.at[pl.ds(64 * b, 64 * nb)], PERM + k)
     phase("send_wait")
     for cp in started:
@@ -557,7 +587,6 @@
     cos, sin = rope_tables()
     any_ = pl.BlockSpec(memory_space=pl.ANY)
     vm = pl.BlockSpec(memory_space=pltpu.VMEM)
-    hbm = pl.BlockSpec(memory_space=pltpu.HBM)
     V = pltpu.VMEM
     prev, gq, go = pl.pallas_call(
         kernel,
@@ -567,7 +596,7 @@
             pltpu.VMEM((128, QKVW), F32),
             pltpu.VMEM((64, D), F32),
         ),
-        in_specs=[any_] * 7 + [hbm] * 2 + [any_] * 2,
+        in_specs=[any_] * 7 + [pl.BlockSpec(memory_space=pltpu.SMEM)] + [any_] * 2,
         out_specs=(vm, vm, vm),
         scratch_shapes=[
             V((2, SEQ, D), BF), V((2, SEQ, D), BF), V((2, SEQ, QW), BF), V((2, SEQ, QKVW), BF),
@@ -577,15 +606,14 @@
             V((2, 128, QKVW), BF), V((2, LOW, D), BF),
             V((2, 2, 128, QKVW), BF), V((2, 2, LOW, D), BF),
             V((128, QKVW), BF), V((LOW, D), BF),
-            V((4, XROWS, D), BF), V((2, XROWS, D // 2), BF), V((2, XROWS, D), BF),
+            V((4, XROWS, D), BF), V((2, XROWS, D // 2), BF), V((2, XROWS, D), BF), V((6, QKVW, 256), BF),
             V((SEQ, D), BF), V((SEQ, 128), F32), V((SEQ, QKVW), F32),
             V((KV_HEADS, 6, 256, 128), BF), V((KV_HEADS, 6, 256, 128), BF),
             V((KV_HEADS, SEQ, 128), BF), V((KV_HEADS, SEQ, 128), BF),
             V((128, QKVW), BF), V((KV_HEADS, SEQ, 128), F32), V((KV_HEADS, SEQ, 128), F32),
             V((128, D), F32), V((128, 128), F32), V((SEQ, D), BF),
             V((1, D), F32), V((SEQ, 128), F32), V((SEQ, 128), F32),
-            pltpu.SMEM((1,), jnp.int32), pltpu.SMEM((1,), jnp.int32),
-            pltpu.SemaphoreType.DMA((11,)),
+            pltpu.SemaphoreType.DMA((9,)),
             pltpu.SemaphoreType.DMA((N_SEM,)),
             pltpu.SemaphoreType.DMA((N_SEM,)),
             pltpu.SemaphoreType.REGULAR,
@@ -594,7 +622,8 @@
             collective_id=0, has_side_effects=True, vmem_limit_bytes=59 * 1024 * 1024
         ),
     )(
-        x[0], g[0], a[0], p[0], wq[0], wo[0], gain, b, w, jnp.asarray(cos), jnp.asarray(sin)
+        x[0], g[0], a[0], p[0], wq[0], wo[0], gain, b + 2 * w,
+        jnp.asarray(cos), jnp.asarray(sin),
     )
     return prev[None], gq[None], go[None]
 

time: 107 us -> 106 us (level)
    pallas_call x1, Pallas kernels: 102 us -> 101 us  [local(): pl.pallas_call(kernel, name='step', out_shape=(pltpu.VMEM((SEQ, D), BF),...]
where the time goes in v4:
time: 106 us
  Pallas kernels  101 us (95%)
  local copies, waits for them, and re-layouts  2.82 us (3%)
  between operations  1.94 us (2%)
    pallas_call x1, Pallas kernels, local(): pl.pallas_call(kernel, name='step', out_shape=(pltpu.VMEM((SEQ, D), BF),...  101 us
    unnamed x3, local copies, waits for them, and re-layouts  2.82 us

profile of v4, /device:TPU:97, one launch (start us, length us, event | category | flops | bytes accessed | tf_op | source)
XLA Modules:
  0.0 105.5 jit_solution(17439292333684009483)
XLA Ops:
  1.9 100.8 %step.1 = (bf16[384,2048]{1,0:T(8,128)(2,1)S(1)}, f32[128,1536]{1,0:T(8,128)S(1)}, f32[64,2048]{1,0:T(8,128)S(1)}) custom-call(bf16[2,384,2048]{2,1,0:T(8,128)(2,1)} %bitcast.12, bf16[2,384,2048]{2,1,0:T(8,128)(2,1)} %bitcast.13, bf16[2,384,1024]{2,1,0:T(8,128)(2,1)} %bitcast.15, bf16[2,384,1536]{2,1,0:T(8,128)(2,1)} %bitcast.14, ...), custom_call_target="tpu_custom_call" | custom-call | tf_op jit(solution)/shard_map/step/pallas_call | solution.py:591
  102.7 1.1 %copy.17 = bf16[1,384,2048]{2,1,0:T(8,128)(2,1)} copy(bf16[1,384,2048]{2,1,0:T(8,128)(2,1)S(1)} %bitcast.9) | data formatting | bytes 3145728
  103.8 0.9 copy.18
  104.7 0.8 copy.19

commit v5 on v4

--- a/solution.py
+++ b/solution.py
@@ -463,7 +463,7 @@
             use(xx * 4 + far, dot(GP[:n], WQ[xx * 4 + far], 1, 1))
             return carry
 
-        lax.fori_loop(0, 6, normed_cols, 0, unroll=2)
+        lax.fori_loop(0, 6, normed_cols, 0, unroll=3)
         lax.fori_loop(0, 2, far_cols, 0, unroll=2)
         phase(f"fin_{b0}")
         inv = INV[rows, :]

time: 106 us -> 105 us (level)
  no operation moved by 1% of the time
where the time goes in v5:
time: 105 us
  Pallas kernels  101 us (96%)
  local copies, waits for them, and re-layouts  2.82 us (3%)
  between operations  1.94 us (2%)
    pallas_call x1, Pallas kernels, local(): pl.pallas_call(kernel, name='step', out_shape=(pltpu.VMEM((SEQ, D), BF),...  101 us
    unnamed x3, local copies, waits for them, and re-layouts  2.82 us

profile of v5, /device:TPU:97, one launch (start us, length us, event | category | flops | bytes accessed | tf_op | source)
XLA Modules:
  0.0 105.4 jit_solution(5390191085458125009)
XLA Ops:
  1.9 100.6 %step.1 = (bf16[384,2048]{1,0:T(8,128)(2,1)S(1)}, f32[128,1536]{1,0:T(8,128)S(1)}, f32[64,2048]{1,0:T(8,128)S(1)}) custom-call(bf16[2,384,2048]{2,1,0:T(8,128)(2,1)} %bitcast.12, bf16[2,384,2048]{2,1,0:T(8,128)(2,1)} %bitcast.13, bf16[2,384,1024]{2,1,0:T(8,128)(2,1)} %bitcast.15, bf16[2,384,1536]{2,1,0:T(8,128)(2,1)} %bitcast.14, ...), custom_call_target="tpu_custom_call" | custom-call | tf_op jit(solution)/shard_map/step/pallas_call | solution.py:591
  102.6 1.1 %copy.17 = bf16[1,384,2048]{2,1,0:T(8,128)(2,1)} copy(bf16[1,384,2048]{2,1,0:T(8,128)(2,1)S(1)} %bitcast.9) | data formatting | bytes 3145728
  103.7 0.9 copy.18
  104.6 0.8 copy.19
